TPU v7x, 32 devices: a whole 2x2x4 slice. The times are simulated.
32 devices in a mesh: gx: 2 (over x), gy: 4 (over y, core), gz: 4 (over z).
Axes of the slice: x: 2, y: 2, z: 4, core: 2. Of those that a mesh axis runs over, the one named last changes fastest.
Arguments:
- conserved: float32 [5, 16, 32, 256], P(None, 'gz', 'gy', 'gx'), may hold values from -3 to 12, as said below
- metrics: float32 [9, 16, 32, 256], P(None, 'gz', 'gy', 'gx'), may hold values from -0.6 to 2, as said below
- inv_volume: float32 [16, 32, 256], P('gz', 'gy', 'gx'), may hold values from 0.5 to 2
- wake_donor: int32 [256], P('gx'), may hold values from -1 to 255, as said below
Outputs:
- section_state: float32 [5, 16, 32, 256], P(None, 'gz', 'gy', 'gx')
- time_rate: float32 [5, 16, 32, 256], P(None, 'gz', 'gy', 'gx')
Inputs may be any that keep to these rules, and one draw needn't show every extreme that they name: `conserved`: each cell holds density rho of 0.5 to 2, pressure p of 0.5 to 2 and velocity components u of -1.5 to 1.5 as (rho, rho u, p / 0.4 + rho |u|^2 / 2). `metrics`: in each cell, row d (entries 3 d to 3 d + 2) has its entry 3 d + d between 0.5 and 2 and its other two entries at most 0.3 times that entry in magnitude. wake_donor[i] is either 256 - 1 - i or -1, and wake_donor[i] >= 0 exactly where wake_donor[255 - i] >= 0.
All inputs are finite; a program needn't handle non-finite values.
Results may differ from a plain program's by a relative error of at most 0.0001.
Values sent between devices are 32-bit elements; how exact they have to be, the bound alone decides.
No kernel may reach another device: no remote copies, remote signals or barrier semaphores. Data moves between devices by JAX's collectives and lax.ppermute only.
A program may use at most 64 MiB of HBM per device.

v0:
```python
import jax
import jax.numpy as jnp
from jax import lax
from jax.sharding import PartitionSpec as P

GAMMA = 1.4
WENO_EPS = 1e-06
STEP_SIZE = 0.08


def from_partner(x, axis, bit):
    return lax.ppermute(x, axis, [(i, i ^ 1 << bit) for i in range(lax.axis_size(axis))])


def padded(block, sides, width, periodic):
    for axis, dim in sides:
        count = lax.axis_size(axis)
        forward = [(i, i + 1) for i in range(count - 1)]
        if periodic:
            forward.append((count - 1, 0))
        backward = [(target, source) for source, target in forward]
        low = lax.ppermute(
            lax.slice_in_dim(block, block.shape[dim] - width, None, axis=dim), axis, forward
        )
        high = lax.ppermute(lax.slice_in_dim(block, 0, width, axis=dim), axis, backward)
        block = jnp.concatenate([low, block, high], axis=dim)
    return block


def slab_of(values, start, amount, axis):
    return lax.slice_in_dim(values, start, start + amount, axis=values.ndim + axis)


def cross_of(first, second):
    return [
        first[1] * second[2] - first[2] * second[1],
        first[2] * second[0] - first[0] * second[2],
        first[0] * second[1] - first[1] * second[0],
    ]


def inner_of(first, second):
    return first[0] * second[0] + first[1] * second[1] + first[2] * second[2]


def cell_terms(fields, metric_row):
    density = fields[0]
    velocity = fields[1:4] / density
    kinetic = 0.5 * jnp.sum(fields[1:4] * velocity, axis=0)
    pressure = (GAMMA - 1.0) * (fields[4] - kinetic)
    contra = jnp.sum(metric_row * velocity, axis=0)
    fluxes = jnp.stack(
        [
            fields[0] * contra,
            fields[1] * contra + metric_row[0] * pressure,
            fields[2] * contra + metric_row[1] * pressure,
            fields[3] * contra + metric_row[2] * pressure,
            (fields[4] + pressure) * contra,
        ]
    )
    sound_speed = jnp.sqrt(GAMMA * pressure / density)
    speeds = jnp.abs(contra) + sound_speed * jnp.sqrt(jnp.sum(metric_row * metric_row, axis=0))
    primitive = jnp.concatenate([density[None], velocity, pressure[None]], axis=0)
    return (primitive, fluxes, speeds)


def eigen_pair(state, metric_row, pick):
    density = state[0]
    velocity = [state[1], state[2], state[3]]
    pressure = state[4]
    row_size = jnp.sqrt(metric_row[0] ** 2 + metric_row[1] ** 2 + metric_row[2] ** 2)
    normal = [metric_row[member] / row_size for member in range(3)]
    axis_unit = [1.0 if member == pick else 0.0 for member in range(3)]
    raw_cross = cross_of(normal, axis_unit)
    raw_size = jnp.sqrt(raw_cross[0] ** 2 + raw_cross[1] ** 2 + raw_cross[2] ** 2)
    tangent = [raw_cross[member] / raw_size for member in range(3)]
    binormal = cross_of(normal, tangent)
    sound_speed = jnp.sqrt(GAMMA * pressure / density)
    inverse = 1.0 / sound_speed
    kinetic = 0.5 * inner_of(velocity, velocity)
    enthalpy = GAMMA / (GAMMA - 1.0) * pressure / density + kinetic
    normal_speed = inner_of(normal, velocity)
    tangent_speed = inner_of(tangent, velocity)
    binormal_speed = inner_of(binormal, velocity)
    factor = (GAMMA - 1.0) * inverse * inverse
    scaled = factor * kinetic
    left_rows = [
        [0.5 * (scaled + normal_speed * inverse)]
        + [0.5 * (-factor * velocity[member] - normal[member] * inverse) for member in range(3)]
        + [0.5 * factor],
        [1.0 - scaled] + [factor * velocity[member] for member in range(3)] + [-factor],
        [-tangent_speed] + tangent + [0.0],
        [-binormal_speed] + binormal + [0.0],
        [0.5 * (scaled - normal_speed * inverse)]
        + [0.5 * (-factor * velocity[member] + normal[member] * inverse) for member in range(3)]
        + [0.5 * factor],
    ]
    right_columns = [
        [1.0]
        + [velocity[member] - sound_speed * normal[member] for member in range(3)]
        + [enthalpy - sound_speed * normal_speed],
        [1.0] + velocity + [kinetic],
        [0.0] + tangent + [tangent_speed],
        [0.0] + binormal + [binormal_speed],
        [1.0]
        + [velocity[member] + sound_speed * normal[member] for member in range(3)]
        + [enthalpy + sound_speed * normal_speed],
    ]
    return (left_rows, right_columns)


def project_left(matrix, vector):
    return jnp.stack(
        [
            sum((matrix[member][second] * vector[second] for second in range(5)))
            for member in range(5)
        ]
    )


def apply_right(matrix, vector):
    return jnp.stack(
        [
            sum((matrix[second][member] * vector[second] for second in range(5)))
            for member in range(5)
        ]
    )


def weno_side(stencil):
    far_left, near_left, center, near_right, far_right = stencil
    guess_zero = (2.0 * far_left - 7.0 * near_left + 11.0 * center) / 6.0
    guess_one = (-near_left + 5.0 * center + 2.0 * near_right) / 6.0
    guess_two = (2.0 * center + 5.0 * near_right - far_right) / 6.0
    smooth_zero = (
        13.0 / 12.0 * (far_left - 2.0 * near_left + center) ** 2
        + 0.25 * (far_left - 4.0 * near_left + 3.0 * center) ** 2
    )
    smooth_one = (
        13.0 / 12.0 * (near_left - 2.0 * center + near_right) ** 2
        + 0.25 * (near_left - near_right) ** 2
    )
    smooth_two = (
        13.0 / 12.0 * (center - 2.0 * near_right + far_right) ** 2
        + 0.25 * (3.0 * center - 4.0 * near_right + far_right) ** 2
    )
    weight_zero = 0.1 / (WENO_EPS + smooth_zero) ** 2
    weight_one = 0.6 / (WENO_EPS + smooth_one) ** 2
    weight_two = 0.3 / (WENO_EPS + smooth_two) ** 2
    return (weight_zero * guess_zero + weight_one * guess_one + weight_two * guess_two) / (
        weight_zero + weight_one + weight_two
    )


def interface_flux(fields, metric_row, axis, pick):
    primitive, fluxes, speeds = cell_terms(fields, metric_row)
    faces_count = fields.shape[fields.ndim + axis] - 5
    mean_state = 0.5 * (
        slab_of(primitive, 2, faces_count, axis) + slab_of(primitive, 3, faces_count, axis)
    )
    mean_row = 0.5 * (
        slab_of(metric_row, 2, faces_count, axis) + slab_of(metric_row, 3, faces_count, axis)
    )
    left_rows, right_columns = eigen_pair(mean_state, mean_row, pick)
    max_speed = slab_of(speeds, 0, faces_count, axis)
    for offset in range(1, 6):
        max_speed = jnp.maximum(max_speed, slab_of(speeds, offset, faces_count, axis))
    upwind = []
    downwind = []
    for offset in range(6):
        state_chars = project_left(left_rows, slab_of(fields, offset, faces_count, axis))
        flux_chars = project_left(left_rows, slab_of(fluxes, offset, faces_count, axis))
        upwind.append(0.5 * (flux_chars + max_speed * state_chars))
        downwind.append(0.5 * (flux_chars - max_speed * state_chars))
    combined = weno_side(upwind[0:5]) + weno_side(downwind[5:0:-1])
    return apply_right(right_columns, combined)


def divergence(fields, metric_row, axis, pick):
    face_flux = interface_flux(fields, metric_row, axis, pick)
    cells_count = face_flux.shape[face_flux.ndim + axis] - 1
    return slab_of(face_flux, 1, cells_count, axis) - slab_of(face_flux, 0, cells_count, axis)


def fix_ends(extended, at_start, at_end):
    interior = extended[..., 3:-3]
    lower_ghost = jnp.where(at_start, jnp.repeat(interior[..., :1], 3, axis=-1), extended[..., :3])
    upper_ghost = jnp.where(at_end, jnp.repeat(interior[..., -1:], 3, axis=-1), extended[..., -3:])
    return jnp.concatenate([lower_ghost, interior, upper_ghost], axis=-1)


def fix_wall(extended, ghosts, at_start, at_end):
    interior = extended[:, :, 3:-3, :]
    lower_ghost = jnp.where(at_start, ghosts, extended[:, :, :3, :])
    upper_ghost = jnp.where(
        at_end, jnp.repeat(interior[:, :, -1:, :], 3, axis=2), extended[:, :, -3:, :]
    )
    return jnp.concatenate([lower_ghost, interior, upper_ghost], axis=2)


def local(conserved, metrics, inv_volume, wake_donor):
    at_inflow = lax.axis_index("gx") == 0
    at_outflow = lax.axis_index("gx") == lax.axis_size("gx") - 1
    at_wall = lax.axis_index("gy") == 0
    at_top = lax.axis_index("gy") == lax.axis_size("gy") - 1
    mirrored = jnp.concatenate([conserved[:, :, 2::-1, :], metrics[3:6, :, 2::-1, :]], axis=0)
    for bit_number in range(lax.axis_size("gx").bit_length() - 1):
        mirrored = from_partner(mirrored, "gx", bit_number)
    mirrored = mirrored[..., ::-1]
    stream_flow, stream_metric = (
        padded(conserved, (("gx", 3),), 3, False),
        padded(metrics, (("gx", 3),), 3, False),
    )
    normal_flow, normal_metric = (
        padded(conserved, (("gy", 2),), 3, False),
        padded(metrics, (("gy", 2),), 3, False),
    )
    span_flow, span_metric = (
        padded(conserved, (("gz", 1),), 3, True),
        padded(metrics, (("gz", 1),), 3, True),
    )
    stream_row = stream_metric[0:3]
    normal_row = normal_metric[3:6]
    span_row = span_metric[6:9]
    stream_flow = fix_ends(stream_flow, at_inflow, at_outflow)
    stream_row = fix_ends(stream_row, at_inflow, at_outflow)
    momentum_sign = jnp.array([1.0, -1.0, -1.0, -1.0, 1.0], dtype=jnp.float32)[:, None, None, None]
    is_wake = wake_donor >= 0
    wake_flow = jnp.where(is_wake, mirrored[0:5], conserved[:, :, 2::-1, :] * momentum_sign)
    wake_row = jnp.where(is_wake, mirrored[5:8], metrics[3:6, :, 2::-1, :])
    normal_flow = fix_wall(normal_flow, wake_flow, at_wall, at_top)
    normal_row = fix_wall(normal_row, wake_row, at_wall, at_top)
    summed = divergence(stream_flow, stream_row, -1, 1)
    summed = summed + divergence(normal_flow, normal_row, -2, 2)
    summed = summed + divergence(span_flow, span_row, -3, 0)
    time_rate = -inv_volume[None] * summed
    return (conserved + STEP_SIZE * time_rate, time_rate)


def solution(mesh):
    placed = (P(None, "gz", "gy", "gx"), P(None, "gz", "gy", "gx"), P("gz", "gy", "gx"), P("gx"))
    return jax.shard_map(
        local,
        mesh=mesh,
        in_specs=placed,
        out_specs=(P(None, "gz", "gy", "gx"), P(None, "gz", "gy", "gx")),
        check_vma=False,
    )
```

profile of v0, /device:TPU:0, one launch (start us, length us, event | category | flops | bytes accessed | tf_op | source)
XLA Modules:
  0.0 47.5 jit_solution(11533834819251356184)
XLA Ops:
  0.6 1.0 %fusion.195 = (f32[5,4,8,3]{3,2,1,0:T(8,128)S(1)}, f32[5,4,8,3]{3,2,1,0:T(8,128)S(1)}) fusion(f32[5,4,8,128]{3,2,1,0:T(8,128)} %param.5), kind=kLoop, calls=%fused_computation.685 | loop fusion | bytes 7680 | tf_op jit(solution)/shard_map/slice | solution.py:25
  1.7 1.3 %collective-permute-start.1 = (f32[5,4,8,3]{3,2,1,0:T(8,128)S(1)}, f32[5,4,8,3]{3,2,1,0:T(8,128)S(1)}, u32[]{:S(2)}, u32[]{:S(2)}) collective-permute-start(f32[5,4,8,3]{3,2,1,0:T(8,128)S(1)} %get-tuple-element.353), channel_id=1, source_target_pairs={{16,0},{17,1},{18,2},{19,3},{20,4},{21,5},{22,6},{23,7},{24,8},{25... | collective-permute-start | bytes 5768 | tf_op jit(solution)/shard_map/ppermute | solution.py:25
  3.0 5.0 %collective-permute-start = (f32[5,4,8,3]{3,2,1,0:T(8,128)S(1)}, f32[5,4,8,3]{3,2,1,0:T(8,128)S(1)}, u32[]{:S(2)}, u32[]{:S(2)}) collective-permute-start(f32[5,4,8,3]{3,2,1,0:T(8,128)S(1)} %get-tuple-element.354), channel_id=1, source_target_pairs={{0,16},{1,17},{2,18},{3,19},{4,20},{5,21},{6,22},{7,23},{8,24},{9,... | collective-permute-start | bytes 5768 | tf_op jit(solution)/shard_map/ppermute | solution.py:22
  8.0 0.1 fusion.191
  8.1 1.3 %collective-permute-start.3 = (f32[9,4,8,3]{3,2,1,0:T(8,128)S(1)}, f32[9,4,8,3]{3,2,1,0:T(8,128)S(1)}, u32[]{:S(2)}, u32[]{:S(2)}) collective-permute-start(f32[9,4,8,3]{3,2,1,0:T(8,128)S(1)} %get-tuple-element.329), channel_id=1, source_target_pairs={{16,0},{17,1},{18,2},{19,3},{20,4},{21,5},{22,6},{23,7},{24,8},{25... | collective-permute-start | bytes 10376 | tf_op jit(solution)/shard_map/ppermute | solution.py:25
  9.4 4.6 %collective-permute-start.2 = (f32[9,4,8,3]{3,2,1,0:T(8,128)S(1)}, f32[9,4,8,3]{3,2,1,0:T(8,128)S(1)}, u32[]{:S(2)}, u32[]{:S(2)}) collective-permute-start(f32[9,4,8,3]{3,2,1,0:T(8,128)S(1)} %get-tuple-element.328), channel_id=1, source_target_pairs={{0,16},{1,17},{2,18},{3,19},{4,20},{5,21},{6,22},{7,23},{8,24},{9,... | collective-permute-start | bytes 10376 | tf_op jit(solution)/shard_map/ppermute | solution.py:22
  14.0 1.3 %collective-permute-start.6 = (f32[5,4,3,128]{3,2,1,0:T(4,128)S(1)}, f32[5,4,3,128]{3,2,1,0:T(4,128)S(1)}, u32[]{:S(2)}, u32[]{:S(2)}) collective-permute-start(f32[5,4,3,128]{3,2,1,0:T(4,128)S(1)} %get-tuple-element.355), channel_id=1, source_target_pairs={{4,0},{8,4},{12,8},{5,1},{9,5},{13,9},{6,2},{10,6},{14,10},{7,3},{... | collective-permute-start | bytes 92168 | tf_op jit(solution)/shard_map/ppermute | solution.py:25
  15.3 0.2 slice_reduce_fusion.1
  15.5 0.2 slice_reduce_fusion.3
  15.9 0.6 %copy-done.4 = s32[128]{0:T(128)S(1)} copy-done((s32[128]{0:T(128)S(1)}, s32[128]{0:T(128)}, u32[]{:S(2)}) %copy-start.4) | copy-done | bytes 536
  16.6 0.7 %copy-done.2 = f32[4,8,128]{2,1,0:T(8,128)S(1)} copy-done((f32[4,8,128]{2,1,0:T(8,128)S(1)}, f32[4,8,128]{2,1,0:T(8,128)}, u32[]{:S(2)}) %copy-start.2) | copy-done | bytes 16408
  17.3 0.1 broadcast_select_fusion
  17.4 3.0 %collective-permute-start.5 = (f32[5,4,3,128]{3,2,1,0:T(4,128)S(1)}, f32[5,4,3,128]{3,2,1,0:T(4,128)S(1)}, u32[]{:S(2)}, u32[]{:S(2)}) collective-permute-start(f32[5,4,3,128]{3,2,1,0:T(4,128)S(1)} %get-tuple-element.356), channel_id=1, source_target_pairs={{0,4},{4,8},{8,12},{1,5},{5,9},{9,13},{2,6},{6,10},{10,14},{3,7},{... | collective-permute-start | bytes 92168 | tf_op jit(solution)/shard_map/ppermute | solution.py:22
  20.4 0.1 broadcast_select_fusion.1
  20.5 0.1 pad_maximum_fusion.1
  20.7 4.2 %collective-permute-start.7 = (f32[9,4,3,128]{3,2,1,0:T(4,128)S(1)}, f32[9,4,3,128]{3,2,1,0:T(4,128)S(1)}, u32[]{:S(2)}, u32[]{:S(2)}) collective-permute-start(f32[9,4,3,128]{3,2,1,0:T(4,128)S(1)} %get-tuple-element.332), channel_id=1, source_target_pairs={{0,4},{4,8},{8,12},{1,5},{5,9},{9,13},{2,6},{6,10},{10,14},{3,7},{... | collective-permute-start | bytes 165896 | tf_op jit(solution)/shard_map/ppermute | solution.py:22
  24.9 0.1 slice_select_fusion
  25.0 1.3 %collective-permute-start.8 = (f32[9,4,3,128]{3,2,1,0:T(4,128)S(1)}, f32[9,4,3,128]{3,2,1,0:T(4,128)S(1)}, u32[]{:S(2)}, u32[]{:S(2)}) collective-permute-start(f32[9,4,3,128]{3,2,1,0:T(4,128)S(1)} %get-tuple-element.333), channel_id=1, source_target_pairs={{4,0},{8,4},{12,8},{5,1},{9,5},{13,9},{6,2},{10,6},{14,10},{7,3},{... | collective-permute-start | bytes 165896 | tf_op jit(solution)/shard_map/ppermute | solution.py:25
  26.3 0.1 slice_select_fusion.1
  26.4 0.1 fusion.15
  26.5 0.1 multiply_reduce_fusion.6
  26.7 0.1 fusion.1
  26.8 0.1 constant_dynamic-update-slice_fusion.9
  27.0 0.1 constant_dynamic-update-slice_fusion.29
  27.1 0.1 constant_dynamic-update-slice_fusion.49
  27.3 0.1 constant_dynamic-update-slice_fusion.19
  27.4 0.1 constant_dynamic-update-slice_fusion.59
  27.6 0.2 constant_dynamic-update-slice_fusion.44
  27.7 0.1 constant_dynamic-update-slice_fusion.4
  27.8 0.2 constant_dynamic-update-slice_fusion.24
  28.0 0.1 slice_maximum_fusion.5
  28.2 0.1 constant_dynamic-update-slice_fusion.7
  28.8 0.2 constant_dynamic-update-slice_fusion.43
  29.0 0.1 constant_dynamic-update-slice_fusion.3
  29.1 0.2 constant_dynamic-update-slice_fusion.52
  29.3 0.1 constant_dynamic-update-slice_fusion.2
  29.4 0.1 constant_dynamic-update-slice_fusion.1
  29.5 0.1 constant_dynamic-update-slice_fusion
  29.6 0.2 constant_dynamic-update-slice_fusion.41
  29.8 0.2 constant_dynamic-update-slice_fusion.40
  30.0 0.2 constant_dynamic-update-slice_fusion.23
  30.1 0.2 constant_dynamic-update-slice_fusion.22
  30.3 0.2 constant_dynamic-update-slice_fusion.21
  30.4 0.2 constant_dynamic-update-slice_fusion.20
  30.6 0.8 %divide_add_fusion.1 = f32[5,4,8,129]{3,2,1,0:T(8,128)S(1)} fusion(f32[5,4,8,129]{3,2,1,0:T(8,128)S(1)} %get-tuple-element.203, f32[5,4,8,129]{3,2,1,0:T(8,128)S(1)} %get-tuple-element.202, f32[5,4,8,129]{3,2,1,0:T(8,128)S(1)} %get-tuple-element.197, f32[5,4,8,129]{3,2,1,0:T(8,128)S(1)} %get-tuple-element.196, f32[5,4,8,129]{3,2,1,0:T(8,128)S(1)} %get-tuple-element.191, ...), kind=kLoop, calls=%fused_computation.333 | loop fusion | flops 3034080 | bytes 1089792 | tf_op jit(solution)/shard_map/add | solution.py:175
  31.6 1.6 %collective-permute-start.9 = (f32[5,3,8,128]{3,2,1,0:T(8,128)S(1)}, f32[5,3,8,128]{3,2,1,0:T(8,128)S(1)}, u32[]{:S(2)}, u32[]{:S(2)}) collective-permute-start(f32[5,3,8,128]{3,2,1,0:T(8,128)S(1)} %get-tuple-element.361), channel_id=1, source_target_pairs={{0,1},{1,2},{2,3},{3,0},{4,5},{5,6},{6,7},{7,4},{8,9},{9,10},{10,1... | collective-permute-start | bytes 184328 | tf_op jit(solution)/shard_map/ppermute | solution.py:22
  33.3 2.3 %collective-permute-start.10 = (f32[5,3,8,128]{3,2,1,0:T(8,128)S(1)}, f32[5,3,8,128]{3,2,1,0:T(8,128)S(1)}, u32[]{:S(2)}, u32[]{:S(2)}) collective-permute-start(f32[5,3,8,128]{3,2,1,0:T(8,128)S(1)} %get-tuple-element.360), channel_id=1, source_target_pairs={{1,0},{2,1},{3,2},{0,3},{5,4},{6,5},{7,6},{4,7},{9,8},{10,9},{11,1... | collective-permute-start | bytes 184328 | tf_op jit(solution)/shard_map/ppermute | solution.py:25
  35.6 0.1 slice.1065
  35.7 0.1 collective-permute-start.11
  35.8 0.6 %copy-done.3 = f32[5]{0:T(128)S(1)} copy-done((f32[5]{0:T(128)S(1)}, f32[5]{0:T(128)}, u32[]{:S(2)}) %copy-start.3) | copy-done | bytes 44
  36.4 0.1 select_select_fusion
  36.5 0.1 slice.1080
  36.6 3.3 %collective-permute-start.12 = (f32[9,3,8,128]{3,2,1,0:T(8,128)S(1)}, f32[9,3,8,128]{3,2,1,0:T(8,128)S(1)}, u32[]{:S(2)}, u32[]{:S(2)}) collective-permute-start(f32[9,3,8,128]{3,2,1,0:T(8,128)S(1)} %get-tuple-element.334), channel_id=1, source_target_pairs={{1,0},{2,1},{3,2},{0,3},{5,4},{6,5},{7,6},{4,7},{9,8},{10,9},{11,1... | collective-permute-start | bytes 331784 | tf_op jit(solution)/shard_map/ppermute | solution.py:25
  40.2 0.1 constant_dynamic-update-slice_fusion.74
  40.6 0.1 constant_dynamic-update-slice_fusion.109
  40.7 0.1 constant_dynamic-update-slice_fusion.89
  41.5 0.1 constant_dynamic-update-slice_fusion.108
  41.9 0.1 constant_dynamic-update-slice_fusion.88
  42.2 0.8 %divide_add_fusion = f32[5,4,9,128]{3,2,1,0:T(8,128)S(1)} fusion(f32[5,4,9,128]{3,2,1,0:T(8,128)S(1)} %get-tuple-element.224, f32[5,4,9,128]{3,2,1,0:T(8,128)S(1)} %get-tuple-element.223, f32[5,4,9,128]{3,2,1,0:T(8,128)S(1)} %get-tuple-element.218, f32[5,4,9,128]{3,2,1,0:T(8,128)S(1)} %get-tuple-element.217, f32[5,4,9,128]{3,2,1,0:T(8,128)S(1)} %get-tuple-element.212, ...), kind=kLoop, calls=%fused_computation.326 | loop fusion | flops 3386880 | bytes 1216512 | tf_op jit(solution)/shard_map/add | solution.py:175
  43.3 0.3 collective-permute-done.11
  43.6 1.1 %collective-permute-done.12 = f32[9,3,8,128]{3,2,1,0:T(8,128)S(1)} collective-permute-done((f32[9,3,8,128]{3,2,1,0:T(8,128)S(1)}, f32[9,3,8,128]{3,2,1,0:T(8,128)S(1)}, u32[]{:S(2)}, u32[]{:S(2)}) %collective-permute-start.12) | collective-permute-done | bytes 110624 | tf_op jit(solution)/shard_map/ppermute | solution.py:25
  44.8 0.1 constant_dynamic-update-slice_fusion.147
  46.1 0.5 %divide_add_fusion.2 = f32[5,5,8,128]{3,2,1,0:T(8,128)S(1)} fusion(f32[5,5,8,128]{3,2,1,0:T(8,128)S(1)} %get-tuple-element.245, f32[5,5,8,128]{3,2,1,0:T(8,128)S(1)} %get-tuple-element.244, f32[5,5,8,128]{3,2,1,0:T(8,128)S(1)} %get-tuple-element.239, f32[5,5,8,128]{3,2,1,0:T(8,128)S(1)} %get-tuple-element.238, f32[5,5,8,128]{3,2,1,0:T(8,128)S(1)} %get-tuple-element.233, ...), kind=kLoop, calls=%fused_computation.346 | loop fusion | flops 3763200 | bytes 1351680 | tf_op jit(solution)/shard_map/add | solution.py:175
  46.7 0.8 %multiply_add_fusion = (f32[5,4,8,128]{3,2,1,0:T(8,128)}, f32[5,4,8,128]{3,2,1,0:T(8,128)}) fusion(f32[5,4,8,128]{3,2,1,0:T(8,128)S(1)} %copy-done, f32[5,5,8,128]{3,2,1,0:T(8,128)S(1)} %constant_dynamic-update-slice_fusion.200, f32[5,4,9,128]{3,2,1,0:T(8,128)S(1)} %constant_dynamic-update-slice_fusion.125, ...), kind=kLoop, calls=%fused_computation.377 | loop fusion | flops 163840 | bytes 753664 | tf_op jit(solution)/shard_map/add | solution.py:237
  (164 shorter events, 4.4 us)
Async XLA Ops:
  0.6 7.4 %copy-start.1 = (f32[9,4,8,128]{3,2,1,0:T(8,128)S(1)}, f32[9,4,8,128]{3,2,1,0:T(8,128)}, u32[]{:S(2)}) copy-start(f32[9,4,8,128]{3,2,1,0:T(8,128)} %param.6) | copy-start | bytes 442372
  1.7 15.6 %collective-permute-start.1 = (f32[5,4,8,3]{3,2,1,0:T(8,128)S(1)}, f32[5,4,8,3]{3,2,1,0:T(8,128)S(1)}, u32[]{:S(2)}, u32[]{:S(2)}) collective-permute-start(f32[5,4,8,3]{3,2,1,0:T(8,128)S(1)} %get-tuple-element.353), channel_id=1, source_target_pairs={{16,0},{17,1},{18,2},{19,3},{20,4},{21,5},{22,6},{23,7},{24,8},{25... | collective-permute-start | bytes 5768 | tf_op jit(solution)/shard_map/ppermute | solution.py:25
  3.0 11.0 %copy-start = (f32[5,4,8,128]{3,2,1,0:T(8,128)S(1)}, f32[5,4,8,128]{3,2,1,0:T(8,128)}, u32[]{:S(2)}) copy-start(f32[5,4,8,128]{3,2,1,0:T(8,128)} %param.5) | copy-start | bytes 245764
  3.0 14.4 %collective-permute-start = (f32[5,4,8,3]{3,2,1,0:T(8,128)S(1)}, f32[5,4,8,3]{3,2,1,0:T(8,128)S(1)}, u32[]{:S(2)}, u32[]{:S(2)}) collective-permute-start(f32[5,4,8,3]{3,2,1,0:T(8,128)S(1)} %get-tuple-element.354), channel_id=1, source_target_pairs={{0,16},{1,17},{2,18},{3,19},{4,20},{5,21},{6,22},{7,23},{8,24},{9,... | collective-permute-start | bytes 5768 | tf_op jit(solution)/shard_map/ppermute | solution.py:22
  8.1 12.6 %collective-permute-start.3 = (f32[9,4,8,3]{3,2,1,0:T(8,128)S(1)}, f32[9,4,8,3]{3,2,1,0:T(8,128)S(1)}, u32[]{:S(2)}, u32[]{:S(2)}) collective-permute-start(f32[9,4,8,3]{3,2,1,0:T(8,128)S(1)} %get-tuple-element.329), channel_id=1, source_target_pairs={{16,0},{17,1},{18,2},{19,3},{20,4},{21,5},{22,6},{23,7},{24,8},{25... | collective-permute-start | bytes 10376 | tf_op jit(solution)/shard_map/ppermute | solution.py:25
  9.4 15.5 %collective-permute-start.2 = (f32[9,4,8,3]{3,2,1,0:T(8,128)S(1)}, f32[9,4,8,3]{3,2,1,0:T(8,128)S(1)}, u32[]{:S(2)}, u32[]{:S(2)}) collective-permute-start(f32[9,4,8,3]{3,2,1,0:T(8,128)S(1)} %get-tuple-element.328), channel_id=1, source_target_pairs={{0,16},{1,17},{2,18},{3,19},{4,20},{5,21},{6,22},{7,23},{8,24},{9,... | collective-permute-start | bytes 10376 | tf_op jit(solution)/shard_map/ppermute | solution.py:22
  14.0 17.6 %collective-permute-start.6 = (f32[5,4,3,128]{3,2,1,0:T(4,128)S(1)}, f32[5,4,3,128]{3,2,1,0:T(4,128)S(1)}, u32[]{:S(2)}, u32[]{:S(2)}) collective-permute-start(f32[5,4,3,128]{3,2,1,0:T(4,128)S(1)} %get-tuple-element.355), channel_id=1, source_target_pairs={{4,0},{8,4},{12,8},{5,1},{9,5},{13,9},{6,2},{10,6},{14,10},{7,3},{... | collective-permute-start | bytes 92168 | tf_op jit(solution)/shard_map/ppermute | solution.py:25
  15.9 0.7 %copy-start.4 = (s32[128]{0:T(128)S(1)}, s32[128]{0:T(128)}, u32[]{:S(2)}) copy-start(s32[128]{0:T(128)} %param.8) | copy-start | bytes 1540
  16.6 0.7 %copy-start.2 = (f32[4,8,128]{2,1,0:T(8,128)S(1)}, f32[4,8,128]{2,1,0:T(8,128)}, u32[]{:S(2)}) copy-start(f32[4,8,128]{2,1,0:T(8,128)} %param.7) | copy-start | bytes 49156
  17.3 16.0 %collective-permute-start.4 = (f32[8,4,3,128]{3,2,1,0:T(4,128)S(1)}, f32[8,4,3,128]{3,2,1,0:T(4,128)S(1)}, u32[]{:S(2)}, u32[]{:S(2)}) collective-permute-start(f32[8,4,3,128]{3,2,1,0:T(4,128)S(1)} %pad_maximum_fusion.11), channel_id=1, source_target_pairs={{0,16},{16,0},{1,17},{17,1},{2,18},{18,2},{3,19},{19,3},{4,20},{20... | collective-permute-start | bytes 147464 | tf_op jit(solution)/shard_map/ppermute | solution.py:12
  17.4 18.3 %collective-permute-start.5 = (f32[5,4,3,128]{3,2,1,0:T(4,128)S(1)}, f32[5,4,3,128]{3,2,1,0:T(4,128)S(1)}, u32[]{:S(2)}, u32[]{:S(2)}) collective-permute-start(f32[5,4,3,128]{3,2,1,0:T(4,128)S(1)} %get-tuple-element.356), channel_id=1, source_target_pairs={{0,4},{4,8},{8,12},{1,5},{5,9},{9,13},{2,6},{6,10},{10,14},{3,7},{... | collective-permute-start | bytes 92168 | tf_op jit(solution)/shard_map/ppermute | solution.py:22
  20.7 15.9 %collective-permute-start.7 = (f32[9,4,3,128]{3,2,1,0:T(4,128)S(1)}, f32[9,4,3,128]{3,2,1,0:T(4,128)S(1)}, u32[]{:S(2)}, u32[]{:S(2)}) collective-permute-start(f32[9,4,3,128]{3,2,1,0:T(4,128)S(1)} %get-tuple-element.332), channel_id=1, source_target_pairs={{0,4},{4,8},{8,12},{1,5},{5,9},{9,13},{2,6},{6,10},{10,14},{3,7},{... | collective-permute-start | bytes 165896 | tf_op jit(solution)/shard_map/ppermute | solution.py:22
  25.0 15.0 %collective-permute-start.8 = (f32[9,4,3,128]{3,2,1,0:T(4,128)S(1)}, f32[9,4,3,128]{3,2,1,0:T(4,128)S(1)}, u32[]{:S(2)}, u32[]{:S(2)}) collective-permute-start(f32[9,4,3,128]{3,2,1,0:T(4,128)S(1)} %get-tuple-element.333), channel_id=1, source_target_pairs={{4,0},{8,4},{12,8},{5,1},{9,5},{13,9},{6,2},{10,6},{14,10},{7,3},{... | collective-permute-start | bytes 165896 | tf_op jit(solution)/shard_map/ppermute | solution.py:25
  31.6 11.6 %collective-permute-start.9 = (f32[5,3,8,128]{3,2,1,0:T(8,128)S(1)}, f32[5,3,8,128]{3,2,1,0:T(8,128)S(1)}, u32[]{:S(2)}, u32[]{:S(2)}) collective-permute-start(f32[5,3,8,128]{3,2,1,0:T(8,128)S(1)} %get-tuple-element.361), channel_id=1, source_target_pairs={{0,1},{1,2},{2,3},{3,0},{4,5},{5,6},{6,7},{7,4},{8,9},{9,10},{10,1... | collective-permute-start | bytes 184328 | tf_op jit(solution)/shard_map/ppermute | solution.py:22
  33.3 10.0 %collective-permute-start.10 = (f32[5,3,8,128]{3,2,1,0:T(8,128)S(1)}, f32[5,3,8,128]{3,2,1,0:T(8,128)S(1)}, u32[]{:S(2)}, u32[]{:S(2)}) collective-permute-start(f32[5,3,8,128]{3,2,1,0:T(8,128)S(1)} %get-tuple-element.360), channel_id=1, source_target_pairs={{1,0},{2,1},{3,2},{0,3},{5,4},{6,5},{7,6},{4,7},{9,8},{10,9},{11,1... | collective-permute-start | bytes 184328 | tf_op jit(solution)/shard_map/ppermute | solution.py:25
  35.7 0.7 %copy-start.3 = (f32[5]{0:T(128)S(1)}, f32[5]{0:T(128)}, u32[]{:S(2)}) copy-start(f32[5]{0:T(128)} %constant.200.clone) | copy-start | bytes 64
  35.7 7.8 %collective-permute-start.11 = (f32[9,3,8,128]{3,2,1,0:T(8,128)S(1)}, f32[9,3,8,128]{3,2,1,0:T(8,128)S(1)}, u32[]{:S(2)}, u32[]{:S(2)}) collective-permute-start(f32[9,3,8,128]{3,2,1,0:T(8,128)S(1)} %get-tuple-element.335), channel_id=1, source_target_pairs={{0,1},{1,2},{2,3},{3,0},{4,5},{5,6},{6,7},{7,4},{8,9},{9,10},{10,1... | collective-permute-start | bytes 331784 | tf_op jit(solution)/shard_map/ppermute | solution.py:22
  36.6 8.0 %collective-permute-start.12 = (f32[9,3,8,128]{3,2,1,0:T(8,128)S(1)}, f32[9,3,8,128]{3,2,1,0:T(8,128)S(1)}, u32[]{:S(2)}, u32[]{:S(2)}) collective-permute-start(f32[9,3,8,128]{3,2,1,0:T(8,128)S(1)} %get-tuple-element.334), channel_id=1, source_target_pairs={{1,0},{2,1},{3,2},{0,3},{5,4},{6,5},{7,6},{4,7},{9,8},{10,9},{11,1... | collective-permute-start | bytes 331784 | tf_op jit(solution)/shard_map/ppermute | solution.py:25
where the time goes:
time: 47.9 us; the launch traced here: 47.5 us
  starting transfers between devices  29.3 us (61%)
  other arithmetic  11.2 us (23%)
  local copies, waits for them, and re-layouts  3.89 us (8%)
  between operations  1.75 us (4%)
  waiting for transfers between devices  1.37 us (3%)
    ppermute x6, starting transfers between devices, padded(): lax.ppermute(lax.slice_in_dim(block, block.shape[dim] - width, None, axis...  18.5 us
    ppermute x6, starting transfers between devices, padded(): lax.ppermute(lax.slice_in_dim(block, 0, width, axis=dim), axis, backward)  10.8 us
    unnamed x100, other arithmetic  5.45 us
    add x3, other arithmetic, interface_flux(): combined = weno_side(upwind[0:5]) + weno_side(downwind[5:0:-1])  2.2 us
    unnamed x14, local copies, waits for them, and re-layouts  1.93 us
    another operation x21, other arithmetic, project_left(): jnp.stack([sum((matrix[member][second] * vector[second] for second in ran...  1.12 us
    ppermute x6, waiting for transfers between devices, padded(): lax.ppermute(lax.slice_in_dim(block, 0, width, axis=dim), axis, backward)  1.08 us
    slice x3, local copies, waits for them, and re-layouts, padded(): lax.slice_in_dim(block, 0, width, axis=dim)  1.07 us
  transfers between devices with their start and end apart: 13, of which 2 were waited for; matrix products, arithmetic and copies ran while one was open for 20% of the time, Pallas kernels for 0%

commit v1 on v0

v1 whole, which is shorter than its diff:
```python
import functools
import jax
import jax.numpy as jnp
from jax import lax
from jax.experimental import pallas as pl
from jax.experimental.pallas import tpu as pltpu
from jax.sharding import PartitionSpec as P

GAMMA = 1.4
EPS4 = 4e-06
STEP_SIZE = 0.08
SLOT = 32


def cell_terms(q, s):
    inv = 1.0 / q[0]
    u = [q[1] * inv, q[2] * inv, q[3] * inv]
    kinetic = 0.5 * (q[1] * u[0] + q[2] * u[1] + q[3] * u[2])
    p = (GAMMA - 1.0) * (q[4] - kinetic)
    contra = s[0] * u[0] + s[1] * u[1] + s[2] * u[2]
    g = [
        q[0] * contra,
        q[1] * contra + s[0] * p,
        q[2] * contra + s[1] * p,
        q[3] * contra + s[2] * p,
        (q[4] + p) * contra,
    ]
    size = s[0] * s[0] + s[1] * s[1] + s[2] * s[2]
    lam = jnp.abs(contra) + jnp.sqrt(GAMMA * p * inv * size)
    return u, p, g, lam


def correction(d, e1, e2, e3):
    base = d * d + EPS4
    b0 = base + e1 * (4.0 / 3.0 * e1 + d)
    b1 = base + e2 * (4.0 / 3.0 * e2 + d)
    d2 = d + e2
    b2 = (d2 * d2 + EPS4) + e3 * (4.0 / 3.0 * e3 - d2)
    b0 = b0 * b0
    b1 = b1 * b1
    b2 = b2 * b2
    x = b2 + b2
    y = 3.0 * b0
    num = b1 * (x * (e1 - e2) + y * (e2 - e3))
    den = b1 * (b2 + y) + x * y
    return num / den


def face_flux(k, rho, u2, p, a, alpha, eq, eg, dq, dg, gsum):
    i, j = (k + 1) % 3, (k + 2) % 3
    u = [0.5 * v for v in u2]
    flat = a[i] * a[i] + a[j] * a[j]
    rn = lax.rsqrt(flat + a[k] * a[k])
    rt = lax.rsqrt(flat)
    n = [v * rn for v in a]
    li, lj = a[j] * rt, -a[i] * rt
    m = [None] * 3
    m[k] = n[i] * lj - n[j] * li
    m[i] = -n[k] * lj
    m[j] = n[k] * li
    c2 = GAMMA * p / rho
    ic = lax.rsqrt(c2)
    kin = 0.5 * (u[0] * u[0] + u[1] * u[1] + u[2] * u[2])
    hic = 0.5 * ic
    nh = [v * hic for v in n]
    hf = 0.2 * ic * ic

    def project(v):
        w = [v[1] - u[0] * v[0], v[2] - u[1] * v[0], v[3] - u[2] * v[0]]
        t = nh[0] * w[0] + nh[1] * w[1] + nh[2] * w[2]
        z = hf * (v[4] - kin * v[0] - (u[0] * w[0] + u[1] * w[1] + u[2] * w[2]))
        return [
            z - t,
            v[0] - (z + z),
            li * w[i] + lj * w[j],
            m[0] * w[0] + m[1] * w[1] + m[2] * w[2],
            z + t,
        ]

    aq = [[alpha * v for v in e] for e in eq]
    ep = [[eg[r][c] + aq[r][c] for c in range(5)] for r in (0, 1, 2)]
    em = [[eg[r][c] - aq[r][c] for c in range(5)] for r in (3, 2, 1)]
    dp = [dg[0][c] + alpha * dq[0][c] for c in range(5)]
    dm = [alpha * dq[1][c] - dg[1][c] for c in range(5)]
    base = [6.0 * gsum[c] - ep[1][c] - em[1][c] for c in range(5)]
    one = [project(v) for v in (dp, ep[0], ep[1], ep[2])]
    two = [project(v) for v in (dm, em[0], em[1], em[2])]
    w = [
        correction(one[0][c], one[1][c], one[2][c], one[3][c])
        + correction(two[0][c], two[1][c], two[2][c], two[3][c])
        for c in range(5)
    ]
    acoustic = w[0] + w[4]
    total = acoustic + w[1]
    dd = (c2 * ic) * (w[4] - w[0])
    y = [n[0] * dd + m[0] * w[3], n[1] * dd + m[1] * w[3], n[2] * dd + m[2] * w[3]]
    y[i] = y[i] + li * w[2]
    y[j] = y[j] + lj * w[2]
    return [
        base[0] + total,
        base[1] + (u[0] * total + y[0]),
        base[2] + (u[1] * total + y[1]),
        base[3] + (u[2] * total + y[2]),
        base[4]
        + (kin * total + 2.5 * c2 * acoustic + (u[0] * y[0] + u[1] * y[1] + u[2] * y[2])),
    ]


def column_fluxes(cells, k):
    terms = [cell_terms(v[:5], v[5:8]) for v in cells]
    q = [v[:5] for v in cells]
    g = [t[2] for t in terms]
    count = len(cells)
    dq = [[q[r + 1][c] - q[r][c] for c in range(5)] for r in range(count - 1)]
    dg = [[g[r + 1][c] - g[r][c] for c in range(5)] for r in range(count - 1)]
    eq = [None] + [[dq[r][c] - dq[r - 1][c] for c in range(5)] for r in range(1, count - 1)]
    eg = [None] + [[dg[r][c] - dg[r - 1][c] for c in range(5)] for r in range(1, count - 1)]
    pair = [jnp.maximum(terms[r][3], terms[r + 1][3]) for r in range(count - 1)]
    out = []
    for f in range(count - 5):
        one, two = f + 2, f + 3
        alpha = jnp.maximum(jnp.maximum(pair[f], pair[f + 2]), pair[f + 4])
        out.append(
            face_flux(
                k,
                q[one][0] + q[two][0],
                [terms[one][0][c] + terms[two][0][c] for c in range(3)],
                terms[one][1] + terms[two][1],
                [cells[one][5 + c] + cells[two][5 + c] for c in range(3)],
                alpha,
                eq[f + 1 : f + 5],
                eg[f + 1 : f + 5],
                (dq[f + 1], dq[f + 3]),
                (dg[f + 1], dg[f + 3]),
                [g[one][c] + g[two][c] for c in range(5)],
            )
        )
    return out


def lane_flux(fields, k):
    lanes = fields[0].shape[1]

    def ahead(v, by):
        return pltpu.roll(v, (-by) % lanes, 1)

    q, s = fields[:5], fields[5:8]
    u, p, g, lam = cell_terms(q, s)

    def stencil(v):
        nxt = ahead(v, 1)
        d = nxt - v
        prev = ahead(d, -1)
        e = d - prev
        e3 = ahead(e, 1)
        return nxt, (prev, d + e3), (ahead(e, -1), e, e3, ahead(e, 2))

    sq = [stencil(v) for v in q]
    sg = [stencil(v) for v in g]
    pair = jnp.maximum(lam, ahead(lam, 1))
    alpha = jnp.maximum(jnp.maximum(pair, ahead(pair, 2)), ahead(pair, -2))
    return face_flux(
        k,
        q[0] + sq[0][0],
        [v + ahead(v, 1) for v in u],
        p + ahead(p, 1),
        [v + ahead(v, 1) for v in s],
        alpha,
        [[v[2][r] for v in sq] for r in range(4)],
        [[v[2][r] for v in sg] for r in range(4)],
        [[v[1][r] for v in sq] for r in range(2)],
        [[v[1][r] for v in sg] for r in range(2)],
        [g[c] + sg[c][0] for c in range(5)],
    )


def field_of(q_ref, s_ref, d, f, rows):
    return q_ref[f, rows, :] if f < 5 else s_ref[3 * d + f - 5, rows, :]


def iotas(shape):
    return lax.broadcasted_iota(jnp.int32, shape, 0), lax.broadcasted_iota(jnp.int32, shape, 1)


def edge_block(q_ref, s_ref, f, cz, cy, cx):
    _, lane = iotas((cy, cx))
    t = lane & (SLOT - 1)
    index = jnp.where(t < 9, jnp.maximum(t - 3, 0), jnp.minimum(t + (cx - 15), cx - 1))
    block = None
    for z in range(cz):
        part = jnp.take_along_axis(
            field_of(q_ref, s_ref, 0, f, pl.ds(z * cy, cy)), index, axis=1
        )
        block = part if block is None else jnp.where(lane >= z * SLOT, part, block)
    return block


def pack_kernel(dims, q_ref, s_ref, za_ref, zb_ref, ya_ref, yb_ref, x_ref, e_ref):
    cz, cy, cx = dims
    half = cy // 2
    row, lane = iotas((cy, cx))
    even_z = lax.rem(lax.axis_index("gz"), 2) == 0
    gy = lax.axis_index("gy")
    even_y = lax.rem(gy, 2) == 0
    top = (cz - 3) * cy
    first_a = pl.multiple_of(jnp.where(even_z, top, 0), cy)
    first_b = pl.multiple_of(jnp.where(even_z, 0, top), cy)
    for f in range(8):
        za_ref[f] = field_of(q_ref, s_ref, 2, f, pl.ds(first_a, 3 * cy))
        zb_ref[f] = field_of(q_ref, s_ref, 2, f, pl.ds(first_b, 3 * cy))
    even_row = (row & 1) == 0
    for f in range(4):
        for i in range(3):
            low = [field_of(q_ref, s_ref, 1, g, pl.ds(i, cy, stride=half)) for g in (f, f + 4)]
            high = [
                field_of(q_ref, s_ref, 1, g, pl.ds(half - 3 + i, cy, stride=half))
                for g in (f, f + 4)
            ]
            low = jnp.where(even_row, low[0], pltpu.roll(low[1], 1, 0))
            high = jnp.where(even_row, pltpu.roll(high[0], cy - 1, 0), high[1])
            ya_ref[f, pl.ds(i * cy, cy), :] = jnp.where(even_y, high, low)
            flipped = jnp.take_along_axis(low, cx - 1 - lane, axis=1)
            low = jnp.where(gy == 0, flipped, low)
            yb_ref[f, pl.ds(i * cy, cy), :] = jnp.where(even_y, low, high)
    blocks = [edge_block(q_ref, s_ref, f, cz, cy, cx) for f in range(8)]
    lower = (lane & (SLOT - 1)) < SLOT // 2
    for f in range(8):
        e_ref[f] = blocks[f]
    for f in range(4):
        x_ref[f] = jnp.where(lower, blocks[f], pltpu.roll(blocks[f + 4], SLOT // 2, 1))


def main_kernel(dims, nx, *refs):
    cz, cy, cx = dims
    half = cy // 2
    q_ref, s_ref, v_ref, w_ref, e_ref, za_ref, zb_ref, ya_ref, yb_ref, xa_ref = refs[:10]
    xb_ref = refs[10] if nx > 2 else xa_ref
    state_ref, rate_ref, acc_ref = refs[-3:]
    row, lane = iotas((cy, cx))
    gx, gy, gz = lax.axis_index("gx"), lax.axis_index("gy"), lax.axis_index("gz")
    even_x, even_y, even_z = lax.rem(gx, 2) == 0, lax.rem(gy, 2) == 0, lax.rem(gz, 2) == 0
    at_wall = gy == 0
    at_top = gy == lax.axis_size("gy") - 1

    t = lane & (SLOT - 1)
    take_low = jnp.logical_and(t < 3, gx > 0)
    take_high = jnp.logical_and(jnp.logical_and(t >= 15, t < 18), gx < nx - 1)
    ends = []
    for f in range(8):
        xa, xb = xa_ref[f % 4], xb_ref[f % 4]
        low = jnp.where(even_x, xb, xa)
        high = jnp.where(even_x, xa, xb)
        shift_low, shift_high = (-12, 12) if f < 4 else (-28, -4)
        low = pltpu.roll(low, shift_low % cx, 1)
        high = pltpu.roll(high, shift_high % cx, 1)
        ends.append(jnp.where(take_low, low, jnp.where(take_high, high, e_ref[f])))
    edge = lane_flux(ends, 1)
    edge = [v - pltpu.roll(v, 1, 1) for v in edge]
    outer = jnp.logical_or(lane < 3, lane >= cx - 3)
    for z in range(cz):
        rows = pl.ds(z * cy, cy)
        flux = lane_flux([field_of(q_ref, s_ref, 0, f, rows) for f in range(8)], 1)
        index = jnp.where(lane < 3, lane + 3, lane - (cx - 3) + 12)
        index = jnp.where(outer, index + z * SLOT, 0)
        for c in range(5):
            inner = flux[c] - pltpu.roll(flux[c], 1, 1)
            outside = jnp.take_along_axis(edge[c], index, axis=1)
            acc_ref[c, rows, :] = jnp.where(outer, outside, inner)

    cells = []
    for r in range(-3, cz + 3):
        fields = []
        for f in range(8):
            if r < 0:
                rows = pl.ds((r + 3) * cy, cy)
                v = jnp.where(even_z, zb_ref[f, rows, :], za_ref[f, rows, :])
            elif r >= cz:
                rows = pl.ds((r - cz) * cy, cy)
                v = jnp.where(even_z, za_ref[f, rows, :], zb_ref[f, rows, :])
            else:
                v = field_of(q_ref, s_ref, 2, f, pl.ds(r * cy, cy))
            fields.append(v)
        cells.append(fields)
    flux = column_fluxes(cells, 0)
    for z in range(cz):
        rows = pl.ds(z * cy, cy)
        for c in range(5):
            acc_ref[c, rows, :] += flux[z + 1][c] - flux[z][c]

    even_row = (row & 1) == 0
    wake = jnp.broadcast_to(w_ref[...] >= 0, (cy, cx))
    own = [
        [field_of(q_ref, s_ref, 1, f, pl.ds(r, cy, stride=half)) for f in range(8)]
        for r in range(half)
    ]
    low_cells, high_cells = [], []
    for i in range(3):
        low_fields, high_fields = [], []
        for f in range(8):
            rows = pl.ds(i * cy, cy)
            back = pl.ds((2 - i) * cy, cy)
            normal = jnp.where(even_y, yb_ref[f % 4, rows, :], ya_ref[f % 4, rows, :])
            mirror = yb_ref[f % 4, back, :]
            low = jnp.where(at_wall, mirror, normal)
            high = jnp.where(even_y, ya_ref[f % 4, rows, :], yb_ref[f % 4, rows, :])
            if f < 4:
                high = pltpu.roll(high, 1, 0)
            else:
                low = pltpu.roll(low, cy - 1, 0)
            solid = own[2 - i][f]
            solid = -solid if f in (1, 2, 3) else solid
            low = jnp.where(jnp.logical_and(at_wall, jnp.logical_not(wake)), solid, low)
            high = jnp.where(at_top, own[half - 1][f], high)
            low_fields.append(jnp.where(even_row, low, pltpu.roll(own[half - 3 + i][f], 1, 0)))
            high_fields.append(jnp.where(even_row, pltpu.roll(own[i][f], cy - 1, 0), high))
        low_cells.append(low_fields)
        high_cells.append(high_fields)
    flux = column_fluxes(low_cells + own + high_cells, 2)
    for r in range(half):
        rows = pl.ds(r, cy, stride=half)
        scale = v_ref[rows, :] * (-1.0 / 12.0)
        for c in range(5):
            rate = scale * (acc_ref[c, rows, :] + (flux[r + 1][c] - flux[r][c]))
            rate_ref[c, rows, :] = rate
            state_ref[c, rows, :] = own[r][c] + STEP_SIZE * rate


def pairs_of(count, shift, wrap):
    found = []
    for i in range(count):
        j = i + 1 if i % 2 == shift else i - 1
        if wrap:
            j %= count
        if 0 <= j < count:
            found.append((i, j))
    return found


def local(dims, sizes, conserved, metrics, inv_volume, wake_donor):
    cz, cy, cx = dims
    nx, ny, nz = sizes
    q = conserved.reshape(5, cz * cy, cx)
    s = metrics.reshape(9, cz * cy, cx)
    v = inv_volume.reshape(cz * cy, cx)
    w = wake_donor.reshape(1, cx)

    def shape(*d):
        return jax.ShapeDtypeStruct(d, jnp.float32)

    za, zb, ya, yb, x, e = pl.pallas_call(
        functools.partial(pack_kernel, dims),
        out_shape=(
            shape(8, 3 * cy, cx),
            shape(8, 3 * cy, cx),
            shape(4, 3 * cy, cx),
            shape(4, 3 * cy, cx),
            shape(4, cy, cx),
            shape(8, cy, cx),
        ),
        name="pack",
    )(q, s)
    second = []
    for a in range(nx):
        second.append((a * ny, (nx - 1 - a) * ny))
        second += [(a * ny + i, a * ny + j) for i, j in pairs_of(ny, 1, False)]
    za = lax.ppermute(za, "gz", pairs_of(nz, 0, True))
    zb = lax.ppermute(zb, "gz", pairs_of(nz, 1, True))
    ya = lax.ppermute(ya, "gy", pairs_of(ny, 0, False))
    yb = lax.ppermute(yb, ("gx", "gy"), second)
    ends = [lax.ppermute(x, "gx", pairs_of(nx, 0, False))]
    if nx > 2:
        ends.append(lax.ppermute(x, "gx", pairs_of(nx, 1, False)))
    state, rate = pl.pallas_call(
        functools.partial(main_kernel, dims, nx),
        out_shape=(shape(5, cz * cy, cx), shape(5, cz * cy, cx)),
        scratch_shapes=[pltpu.VMEM((5, cz * cy, cx), jnp.float32)],
        name="section",
    )(q, s, v, w, e, za, zb, ya, yb, *ends)
    return state.reshape(conserved.shape), rate.reshape(conserved.shape)


def solution(mesh):
    sizes = (mesh.shape["gx"], mesh.shape["gy"], mesh.shape["gz"])
    placed = (P(None, "gz", "gy", "gx"), P(None, "gz", "gy", "gx"), P("gz", "gy", "gx"), P("gx"))

    def block(conserved, metrics, inv_volume, wake_donor):
        return local(inv_volume.shape, sizes, conserved, metrics, inv_volume, wake_donor)

    return jax.shard_map(
        block,
        mesh=mesh,
        in_specs=placed,
        out_specs=(P(None, "gz", "gy", "gx"), P(None, "gz", "gy", "gx")),
        check_vma=False,
    )
```

time: 47.9 us -> 20.5 us (0.43)
  starting transfers between devices: 29.3 us -> 9.52 us
  other arithmetic: 11.2 us -> 0 us
  Pallas kernels: 0 us -> 5.99 us
  local copies, waits for them, and re-layouts: 3.89 us -> 0.66 us
  waiting for transfers between devices: 1.37 us -> 3.42 us
  between operations: 1.75 us -> 0.69 us
    ppermute x13 -> x5, starting transfers between devices: 29.3 us -> 9.52 us  [the longest x1 3.39 us: local(): yb = lax.ppermute(yb, ('gx', 'gy'), second)]
    pallas_call x0 -> x2, Pallas kernels: none -> 5.99 us  [the longest x1 4.23 us: local(): pl.pallas_call(functools.partial(main_kernel, dims, nx), out_shape=(shape...]
    unnamed x100 -> x0, other arithmetic: 5.45 us -> none
    add x10 -> x0, other arithmetic: 3.16 us -> none  [the longest x3 2.2 us: interface_flux(): combined = weno_side(upwind[0:5]) + weno_side(downwind[5:0:-1])]
    ppermute x13 -> x5, waiting for transfers between devices: 1.37 us -> 3.42 us  [the longest x1 3.41 us: local(): ends = [lax.ppermute(x, 'gx', pairs_of(nx, 0, False))]]
    slice x16 -> x0, local copies, waits for them, and re-layouts: 1.84 us -> none  [the longest x3 1.07 us: padded(): lax.slice_in_dim(block, 0, width, axis=dim)]
    unnamed x14 -> x10, local copies, waits for them, and re-layouts: 1.93 us -> 0.66 us
    another operation x24 -> x0, other arithmetic: 1.25 us -> none  [the longest x21 1.12 us: project_left(): jnp.stack([sum((matrix[member][second] * vector[second] for second in ran...]
  transfers between devices with their start and end apart: 13 -> 5, of which waited for: 2 -> 1; matrix products, arithmetic and copies ran while one was open for 20% -> 0% of each run, Pallas kernels for 0% -> 0%
where the time goes in v1:
time: 20.5 us; the launch traced here: 20.3 us
  starting transfers between devices  9.52 us (46%)
  Pallas kernels  5.99 us (29%)
  waiting for transfers between devices  3.42 us (17%)
  between operations  0.69 us (3%)
  local copies, waits for them, and re-layouts  0.66 us (3%)
    pallas_call x1, Pallas kernels, local(): pl.pallas_call(functools.partial(main_kernel, dims, nx), out_shape=(shape...  4.23 us
    ppermute x1, waiting for transfers between devices, local(): ends = [lax.ppermute(x, 'gx', pairs_of(nx, 0, False))]  3.41 us
    ppermute x1, starting transfers between devices, local(): yb = lax.ppermute(yb, ('gx', 'gy'), second)  3.39 us
    ppermute x1, starting transfers between devices, local(): za = lax.ppermute(za, 'gz', pairs_of(nz, 0, True))  3.05 us
    ppermute x1, starting transfers between devices, local(): zb = lax.ppermute(zb, 'gz', pairs_of(nz, 1, True))  2.48 us
    pallas_call x1, Pallas kernels, local(): pl.pallas_call(functools.partial(pack_kernel, dims), out_shape=(shape(8,...  1.76 us
    unnamed x10, local copies, waits for them, and re-layouts  0.66 us
    ppermute x1, starting transfers between devices, local(): ends = [lax.ppermute(x, 'gx', pairs_of(nx, 0, False))]  0.6 us
  transfers between devices with their start and end apart: 5, of which 1 were waited for; matrix products, arithmetic and copies ran while one was open for 0% of the time, Pallas kernels for 0%

profile of v1, /device:TPU:0, one launch (start us, length us, event | category | flops | bytes accessed | tf_op | source)
XLA Modules:
  0.0 20.3 jit_solution(11309101328325911002)
XLA Ops:
  0.6 1.8 %pack.1 = (f32[8,24,128]{2,1,0:T(8,128)}, f32[8,24,128]{2,1,0:T(8,128)}, f32[4,24,128]{2,1,0:T(8,128)}, f32[4,24,128]{2,1,0:T(8,128)}, f32[4,8,128]{2,1,0:T(8,128)}, /*index=5*/f32[8,8,128]{2,1,0:T(8,128)}) custom-call(f32[5,32,128]{2,1,0:T(8,128)} %bitcast.8, f32[9,32,128]{2,1,0:T(8,128)} %bitcast.6), custom_call_target="tpu_custom_call" | custom-call | tf_op jit(solution)/shard_map/pack/pallas_call | solution.py:350
  2.4 3.1 %collective-permute-start = (f32[8,24,128]{2,1,0:T(8,128)}, f32[8,24,128]{2,1,0:T(8,128)S(1)}, u32[]{:S(2)}, u32[]{:S(2)}) collective-permute-start(f32[8,24,128]{2,1,0:T(8,128)} %get-tuple-element.11), channel_id=1, source_target_pairs={{0,1},{1,0},{2,3},{3,2},{4,5},{5,4},{6,7},{7,6},{8,9},{9,8},{10,11... | collective-permute-start | bytes 294920 | tf_op jit(solution)/shard_map/ppermute | solution.py:366
  5.4 2.5 %collective-permute-start.1 = (f32[8,24,128]{2,1,0:T(8,128)}, f32[8,24,128]{2,1,0:T(8,128)S(1)}, u32[]{:S(2)}, u32[]{:S(2)}) collective-permute-start(f32[8,24,128]{2,1,0:T(8,128)} %get-tuple-element.12), channel_id=1, source_target_pairs={{0,3},{1,2},{2,1},{3,0},{4,7},{5,6},{6,5},{7,4},{8,11},{9,10},{10,... | collective-permute-start | bytes 294920 | tf_op jit(solution)/shard_map/ppermute | solution.py:367
  7.9 0.0 collective-permute-start.2
  7.9 3.4 %collective-permute-start.3 = (f32[4,24,128]{2,1,0:T(8,128)}, f32[4,24,128]{2,1,0:T(8,128)S(1)}, u32[]{:S(2)}, u32[]{:S(2)}) collective-permute-start(f32[4,24,128]{2,1,0:T(8,128)} %get-tuple-element.14), channel_id=1, source_target_pairs={{0,16},{4,8},{8,4},{16,0},{20,24},{24,20},{1,17},{5,9},{9,5},{17,1... | collective-permute-start | bytes 147464 | tf_op jit(solution)/shard_map/ppermute | solution.py:369
  11.3 0.6 %collective-permute-start.4 = (f32[4,8,128]{2,1,0:T(8,128)}, f32[4,8,128]{2,1,0:T(8,128)S(1)}, u32[]{:S(2)}, u32[]{:S(2)}) collective-permute-start(f32[4,8,128]{2,1,0:T(8,128)} %get-tuple-element.15), channel_id=1, source_target_pairs={{0,16},{16,0},{1,17},{17,1},{2,18},{18,2},{3,19},{19,3},{4,20},{20... | collective-permute-start | bytes 49160 | tf_op jit(solution)/shard_map/ppermute | solution.py:370
  11.9 3.4 %collective-permute-done.4.refs_9_ = f32[4,8,128]{2,1,0:T(8,128)S(1)} collective-permute-done((f32[4,8,128]{2,1,0:T(8,128)}, f32[4,8,128]{2,1,0:T(8,128)S(1)}, u32[]{:S(2)}, u32[]{:S(2)}) %collective-permute-start.4) | collective-permute-done | bytes 16416 | tf_op jit(solution)/shard_map/ppermute | solution.py:370
  15.3 0.0 copy-start.4
  15.3 0.0 collective-permute-done.2.refs_7_
  15.3 0.0 copy-start.2
  15.3 0.0 collective-permute-done.3.refs_8_
  15.3 0.0 copy-start.3
  15.4 0.0 collective-permute-done.refs_5_
  15.4 0.0 copy-start
  15.4 0.0 collective-permute-done.1.refs_6_
  15.4 0.0 copy-start.1
  15.4 0.5 %copy-done.4 = f32[4,8,128]{2,1,0:T(8,128)} copy-done((f32[4,8,128]{2,1,0:T(8,128)}, f32[4,8,128]{2,1,0:T(8,128)S(1)}, u32[]{:S(2)}) %copy-start.4) | copy-done | bytes 16408
  15.9 0.0 copy-done.2
  16.0 0.0 copy-done.3
  16.0 0.0 copy-done
  16.0 0.0 copy-done.1
  16.0 4.2 %section.1 = (f32[5,32,128]{2,1,0:T(8,128)}, f32[5,32,128]{2,1,0:T(8,128)}) custom-call(f32[5,32,128]{2,1,0:T(8,128)} %bitcast.9, f32[9,32,128]{2,1,0:T(8,128)} %bitcast.7, f32[32,128]{1,0:T(8,128)} %bitcast.10, s32[1,128]{1,0:T(1,128)} %bitcast.11, f32[8,8,128]{2,1,0:T(8,128)} %get-tuple-element.10.refs_4_, f32[8,24,128]{2,1,0:T(8,128)} %copy-done, ...), custom_call_target="tpu_custom_call" | custom-call | tf_op jit(solution)/shard_map/section/pallas_call | solution.py:373
Async XLA Ops:
  2.4 13.0 %collective-permute-start = (f32[8,24,128]{2,1,0:T(8,128)}, f32[8,24,128]{2,1,0:T(8,128)S(1)}, u32[]{:S(2)}, u32[]{:S(2)}) collective-permute-start(f32[8,24,128]{2,1,0:T(8,128)} %get-tuple-element.11), channel_id=1, source_target_pairs={{0,1},{1,0},{2,3},{3,2},{4,5},{5,4},{6,7},{7,6},{8,9},{9,8},{10,11... | collective-permute-start | bytes 294920 | tf_op jit(solution)/shard_map/ppermute | solution.py:366
  5.4 9.9 %collective-permute-start.1 = (f32[8,24,128]{2,1,0:T(8,128)}, f32[8,24,128]{2,1,0:T(8,128)S(1)}, u32[]{:S(2)}, u32[]{:S(2)}) collective-permute-start(f32[8,24,128]{2,1,0:T(8,128)} %get-tuple-element.12), channel_id=1, source_target_pairs={{0,3},{1,2},{2,1},{3,0},{4,7},{5,6},{6,5},{7,4},{8,11},{9,10},{10,... | collective-permute-start | bytes 294920 | tf_op jit(solution)/shard_map/ppermute | solution.py:367
  7.9 7.4 %collective-permute-start.2 = (f32[4,24,128]{2,1,0:T(8,128)}, f32[4,24,128]{2,1,0:T(8,128)S(1)}, u32[]{:S(2)}, u32[]{:S(2)}) collective-permute-start(f32[4,24,128]{2,1,0:T(8,128)} %get-tuple-element.13), channel_id=1, source_target_pairs={{0,4},{4,0},{8,12},{12,8},{1,5},{5,1},{9,13},{13,9},{2,6},{6,2},{1... | collective-permute-start | bytes 147464 | tf_op jit(solution)/shard_map/ppermute | solution.py:368
  7.9 7.4 %collective-permute-start.3 = (f32[4,24,128]{2,1,0:T(8,128)}, f32[4,24,128]{2,1,0:T(8,128)S(1)}, u32[]{:S(2)}, u32[]{:S(2)}) collective-permute-start(f32[4,24,128]{2,1,0:T(8,128)} %get-tuple-element.14), channel_id=1, source_target_pairs={{0,16},{4,8},{8,4},{16,0},{20,24},{24,20},{1,17},{5,9},{9,5},{17,1... | collective-permute-start | bytes 147464 | tf_op jit(solution)/shard_map/ppermute | solution.py:369
  11.3 4.0 %collective-permute-start.4 = (f32[4,8,128]{2,1,0:T(8,128)}, f32[4,8,128]{2,1,0:T(8,128)S(1)}, u32[]{:S(2)}, u32[]{:S(2)}) collective-permute-start(f32[4,8,128]{2,1,0:T(8,128)} %get-tuple-element.15), channel_id=1, source_target_pairs={{0,16},{16,0},{1,17},{17,1},{2,18},{18,2},{3,19},{19,3},{4,20},{20... | collective-permute-start | bytes 49160 | tf_op jit(solution)/shard_map/ppermute | solution.py:370
  15.3 0.6 %copy-start.4 = (f32[4,8,128]{2,1,0:T(8,128)}, f32[4,8,128]{2,1,0:T(8,128)S(1)}, u32[]{:S(2)}) copy-start(f32[4,8,128]{2,1,0:T(8,128)S(1)} %collective-permute-done.4.refs_9_) | copy-start | bytes 49156
  15.3 0.6 %copy-start.2 = (f32[4,24,128]{2,1,0:T(8,128)}, f32[4,24,128]{2,1,0:T(8,128)S(1)}, u32[]{:S(2)}) copy-start(f32[4,24,128]{2,1,0:T(8,128)S(1)} %collective-permute-done.2.refs_7_) | copy-start | bytes 147460
  15.3 0.6 %copy-start.3 = (f32[4,24,128]{2,1,0:T(8,128)}, f32[4,24,128]{2,1,0:T(8,128)S(1)}, u32[]{:S(2)}) copy-start(f32[4,24,128]{2,1,0:T(8,128)S(1)} %collective-permute-done.3.refs_8_) | copy-start | bytes 147460
  15.4 0.7 %copy-start = (f32[8,24,128]{2,1,0:T(8,128)}, f32[8,24,128]{2,1,0:T(8,128)S(1)}, u32[]{:S(2)}) copy-start(f32[8,24,128]{2,1,0:T(8,128)S(1)} %collective-permute-done.refs_5_) | copy-start | bytes 294916
  15.4 0.7 %copy-start.1 = (f32[8,24,128]{2,1,0:T(8,128)}, f32[8,24,128]{2,1,0:T(8,128)S(1)}, u32[]{:S(2)}) copy-start(f32[8,24,128]{2,1,0:T(8,128)S(1)} %collective-permute-done.1.refs_6_) | copy-start | bytes 294916

commit v2 on v1

--- a/solution.py
+++ b/solution.py
@@ -357,6 +357,7 @@
             shape(4, cy, cx),
             shape(8, cy, cx),
         ),
+        compiler_params=pltpu.CompilerParams(vmem_limit_bytes=4 * 2**20),
         name="pack",
     )(q, s)
     second = []
@@ -374,6 +375,7 @@
         functools.partial(main_kernel, dims, nx),
         out_shape=(shape(5, cz * cy, cx), shape(5, cz * cy, cx)),
         scratch_shapes=[pltpu.VMEM((5, cz * cy, cx), jnp.float32)],
+        compiler_params=pltpu.CompilerParams(vmem_limit_bytes=8 * 2**20),
         name="section",
     )(q, s, v, w, e, za, zb, ya, yb, *ends)
     return state.reshape(conserved.shape), rate.reshape(conserved.shape)

time: 20.5 us -> 20.1 us (0.980)
  Pallas kernels: 5.99 us -> 3.27 us
  local copies, waits for them, and re-layouts: 0.66 us -> 3.14 us
  waiting for transfers between devices: 3.42 us -> 3.21 us
    unnamed x10 -> x12, local copies, waits for them, and re-layouts: 0.66 us -> 3.14 us
    pallas_call x1, Pallas kernels: 1.76 us -> 0.17 us  [local(): pl.pallas_call(functools.partial(pack_kernel, dims), out_shape=(shape(8,...]
    pallas_call x1, Pallas kernels: 4.23 us -> 3.1 us  [local(): pl.pallas_call(functools.partial(main_kernel, dims, nx), out_shape=(shape...]
    ppermute x1, waiting for transfers between devices: 3.41 us -> 3.2 us  [local(): ends = [lax.ppermute(x, 'gx', pairs_of(nx, 0, False))]]
where the time goes in v2:
time: 20.1 us; the launch traced here: 19.9 us
  starting transfers between devices  9.54 us (47%)
  Pallas kernels  3.27 us (16%)
  waiting for transfers between devices  3.21 us (16%)
  local copies, waits for them, and re-layouts  3.14 us (16%)
  between operations  0.69 us (3%)
    ppermute x1, starting transfers between devices, local(): yb = lax.ppermute(yb, ('gx', 'gy'), second)  3.39 us
    ppermute x1, waiting for transfers between devices, local(): ends = [lax.ppermute(x, 'gx', pairs_of(nx, 0, False))]  3.2 us
    unnamed x12, local copies, waits for them, and re-layouts  3.14 us
    pallas_call x1, Pallas kernels, local(): pl.pallas_call(functools.partial(main_kernel, dims, nx), out_shape=(shape...  3.1 us
    ppermute x1, starting transfers between devices, local(): za = lax.ppermute(za, 'gz', pairs_of(nz, 0, True))  3.08 us
    ppermute x1, starting transfers between devices, local(): zb = lax.ppermute(zb, 'gz', pairs_of(nz, 1, True))  2.47 us
    ppermute x1, starting transfers between devices, local(): ends = [lax.ppermute(x, 'gx', pairs_of(nx, 0, False))]  0.6 us
  transfers between devices with their start and end apart: 5, of which 1 were waited for; matrix products, arithmetic and copies ran while one was open for 0% of the time, Pallas kernels for 0%

profile of v2, /device:TPU:0, one launch (start us, length us, event | category | flops | bytes accessed | tf_op | source)
XLA Modules:
  0.0 19.9 jit_solution(16639337246753805710)
XLA Ops:
  0.6 0.0 copy-start
  0.6 0.9 %copy-done = f32[9,4,8,128]{3,2,1,0:T(8,128)S(1)} copy-done((f32[9,4,8,128]{3,2,1,0:T(8,128)S(1)}, f32[9,4,8,128]{3,2,1,0:T(8,128)}, u32[]{:S(2)}) %copy-start) | copy-done | bytes 147480
  1.5 0.0 copy-start.2
  1.5 0.9 %copy-done.2 = f32[5,4,8,128]{3,2,1,0:T(8,128)S(1)} copy-done((f32[5,4,8,128]{3,2,1,0:T(8,128)S(1)}, f32[5,4,8,128]{3,2,1,0:T(8,128)}, u32[]{:S(2)}) %copy-start.2) | copy-done | bytes 81944
  2.4 0.0 copy-start.1
  2.4 0.0 copy-start.3
  2.4 0.2 pack.1
  2.6 3.1 %collective-permute-start = (f32[8,24,128]{2,1,0:T(8,128)S(1)}, f32[8,24,128]{2,1,0:T(8,128)S(1)}, u32[]{:S(2)}, u32[]{:S(2)}) collective-permute-start(f32[8,24,128]{2,1,0:T(8,128)S(1)} %get-tuple-element.11), channel_id=1, source_target_pairs={{0,1},{1,0},{2,3},{3,2},{4,5},{5,4},{6,7},{7,6},{8,9},{9,8},{10,11... | collective-permute-start | bytes 294920 | tf_op jit(solution)/shard_map/ppermute | solution.py:367
  5.7 2.5 %collective-permute-start.1 = (f32[8,24,128]{2,1,0:T(8,128)S(1)}, f32[8,24,128]{2,1,0:T(8,128)S(1)}, u32[]{:S(2)}, u32[]{:S(2)}) collective-permute-start(f32[8,24,128]{2,1,0:T(8,128)S(1)} %get-tuple-element.12), channel_id=1, source_target_pairs={{0,3},{1,2},{2,1},{3,0},{4,7},{5,6},{6,5},{7,4},{8,11},{9,10},{10,... | collective-permute-start | bytes 294920 | tf_op jit(solution)/shard_map/ppermute | solution.py:368
  8.2 0.0 collective-permute-start.2
  8.2 3.4 %collective-permute-start.3 = (f32[4,24,128]{2,1,0:T(8,128)S(1)}, f32[4,24,128]{2,1,0:T(8,128)S(1)}, u32[]{:S(2)}, u32[]{:S(2)}) collective-permute-start(f32[4,24,128]{2,1,0:T(8,128)S(1)} %get-tuple-element.14), channel_id=1, source_target_pairs={{0,16},{4,8},{8,4},{16,0},{20,24},{24,20},{1,17},{5,9},{9,5},{17,1... | collective-permute-start | bytes 147464 | tf_op jit(solution)/shard_map/ppermute | solution.py:370
  11.6 0.6 %collective-permute-start.4 = (f32[4,8,128]{2,1,0:T(8,128)S(1)}, f32[4,8,128]{2,1,0:T(8,128)S(1)}, u32[]{:S(2)}, u32[]{:S(2)}) collective-permute-start(f32[4,8,128]{2,1,0:T(8,128)S(1)} %get-tuple-element.15), channel_id=1, source_target_pairs={{0,16},{16,0},{1,17},{17,1},{2,18},{18,2},{3,19},{19,3},{4,20},{20... | collective-permute-start | bytes 49160 | tf_op jit(solution)/shard_map/ppermute | solution.py:371
  12.2 3.2 %collective-permute-done.4.refs_9_ = f32[4,8,128]{2,1,0:T(8,128)S(1)} collective-permute-done((f32[4,8,128]{2,1,0:T(8,128)S(1)}, f32[4,8,128]{2,1,0:T(8,128)S(1)}, u32[]{:S(2)}, u32[]{:S(2)}) %collective-permute-start.4) | collective-permute-done | bytes 16416 | tf_op jit(solution)/shard_map/ppermute | solution.py:371
  15.4 0.0 collective-permute-done.2.refs_7_
  15.4 0.0 collective-permute-done.3.refs_8_
  15.4 0.0 collective-permute-done.refs_5_
  15.4 0.0 collective-permute-done.1.refs_6_
  15.4 0.0 copy-start.5
  15.4 0.0 copy-done.1
  15.4 0.0 copy-done.3
  15.4 0.6 %copy-done.5 = s32[128]{0:T(128)S(1)} copy-done((s32[128]{0:T(128)S(1)}, s32[128]{0:T(128)}, u32[]{:S(2)}) %copy-start.5) | copy-done | bytes 536
  16.0 0.0 copy-start.4
  16.0 0.7 %copy-done.4 = f32[4,8,128]{2,1,0:T(8,128)S(1)} copy-done((f32[4,8,128]{2,1,0:T(8,128)S(1)}, f32[4,8,128]{2,1,0:T(8,128)}, u32[]{:S(2)}) %copy-start.4) | copy-done | bytes 16408
  16.8 3.1 %section.1 = (f32[5,32,128]{2,1,0:T(8,128)}, f32[5,32,128]{2,1,0:T(8,128)}) custom-call(f32[5,32,128]{2,1,0:T(8,128)S(1)} %bitcast.9, f32[9,32,128]{2,1,0:T(8,128)S(1)} %bitcast.7, f32[32,128]{1,0:T(8,128)S(1)} %bitcast.10, s32[1,128]{1,0:T(1,128)S(1)} %bitcast.11, f32[8,8,128]{2,1,0:T(8,128)S(1)} %get-tuple-element.10.refs_4_, ...), custom_call_target="tpu_custom_call" | custom-call | tf_op jit(solution)/shard_map/section/pallas_call | solution.py:374
Async XLA Ops:
  0.6 0.9 %copy-start = (f32[9,4,8,128]{3,2,1,0:T(8,128)S(1)}, f32[9,4,8,128]{3,2,1,0:T(8,128)}, u32[]{:S(2)}) copy-start(f32[9,4,8,128]{3,2,1,0:T(8,128)} %param.5) | copy-start | bytes 442372
  1.5 0.9 %copy-start.2 = (f32[5,4,8,128]{3,2,1,0:T(8,128)S(1)}, f32[5,4,8,128]{3,2,1,0:T(8,128)}, u32[]{:S(2)}) copy-start(f32[5,4,8,128]{3,2,1,0:T(8,128)} %param.4) | copy-start | bytes 245764
  2.4 13.0 %copy-start.1 = (f32[9,4,8,128]{3,2,1,0:T(8,128)S(1)}, f32[9,4,8,128]{3,2,1,0:T(8,128)}, u32[]{:S(2)}) copy-start(f32[9,4,8,128]{3,2,1,0:T(8,128)} %param.5) | copy-start | bytes 442372
  2.4 13.0 %copy-start.3 = (f32[5,4,8,128]{3,2,1,0:T(8,128)S(1)}, f32[5,4,8,128]{3,2,1,0:T(8,128)}, u32[]{:S(2)}) copy-start(f32[5,4,8,128]{3,2,1,0:T(8,128)} %param.4) | copy-start | bytes 245764
  2.6 12.8 %collective-permute-start = (f32[8,24,128]{2,1,0:T(8,128)S(1)}, f32[8,24,128]{2,1,0:T(8,128)S(1)}, u32[]{:S(2)}, u32[]{:S(2)}) collective-permute-start(f32[8,24,128]{2,1,0:T(8,128)S(1)} %get-tuple-element.11), channel_id=1, source_target_pairs={{0,1},{1,0},{2,3},{3,2},{4,5},{5,4},{6,7},{7,6},{8,9},{9,8},{10,11... | collective-permute-start | bytes 294920 | tf_op jit(solution)/shard_map/ppermute | solution.py:367
  5.7 9.7 %collective-permute-start.1 = (f32[8,24,128]{2,1,0:T(8,128)S(1)}, f32[8,24,128]{2,1,0:T(8,128)S(1)}, u32[]{:S(2)}, u32[]{:S(2)}) collective-permute-start(f32[8,24,128]{2,1,0:T(8,128)S(1)} %get-tuple-element.12), channel_id=1, source_target_pairs={{0,3},{1,2},{2,1},{3,0},{4,7},{5,6},{6,5},{7,4},{8,11},{9,10},{10,... | collective-permute-start | bytes 294920 | tf_op jit(solution)/shard_map/ppermute | solution.py:368
  8.2 7.2 %collective-permute-start.2 = (f32[4,24,128]{2,1,0:T(8,128)S(1)}, f32[4,24,128]{2,1,0:T(8,128)S(1)}, u32[]{:S(2)}, u32[]{:S(2)}) collective-permute-start(f32[4,24,128]{2,1,0:T(8,128)S(1)} %get-tuple-element.13), channel_id=1, source_target_pairs={{0,4},{4,0},{8,12},{12,8},{1,5},{5,1},{9,13},{13,9},{2,6},{6,2},{1... | collective-permute-start | bytes 147464 | tf_op jit(solution)/shard_map/ppermute | solution.py:369
  8.2 7.2 %collective-permute-start.3 = (f32[4,24,128]{2,1,0:T(8,128)S(1)}, f32[4,24,128]{2,1,0:T(8,128)S(1)}, u32[]{:S(2)}, u32[]{:S(2)}) collective-permute-start(f32[4,24,128]{2,1,0:T(8,128)S(1)} %get-tuple-element.14), channel_id=1, source_target_pairs={{0,16},{4,8},{8,4},{16,0},{20,24},{24,20},{1,17},{5,9},{9,5},{17,1... | collective-permute-start | bytes 147464 | tf_op jit(solution)/shard_map/ppermute | solution.py:370
  11.6 3.8 %collective-permute-start.4 = (f32[4,8,128]{2,1,0:T(8,128)S(1)}, f32[4,8,128]{2,1,0:T(8,128)S(1)}, u32[]{:S(2)}, u32[]{:S(2)}) collective-permute-start(f32[4,8,128]{2,1,0:T(8,128)S(1)} %get-tuple-element.15), channel_id=1, source_target_pairs={{0,16},{16,0},{1,17},{17,1},{2,18},{18,2},{3,19},{19,3},{4,20},{20... | collective-permute-start | bytes 49160 | tf_op jit(solution)/shard_map/ppermute | solution.py:371
  15.4 0.7 %copy-start.5 = (s32[128]{0:T(128)S(1)}, s32[128]{0:T(128)}, u32[]{:S(2)}) copy-start(s32[128]{0:T(128)} %param.7) | copy-start | bytes 1540
  16.0 0.7 %copy-start.4 = (f32[4,8,128]{2,1,0:T(8,128)S(1)}, f32[4,8,128]{2,1,0:T(8,128)}, u32[]{:S(2)}) copy-start(f32[4,8,128]{2,1,0:T(8,128)} %param.6) | copy-start | bytes 49156

commit v3 on v1

--- a/solution.py
+++ b/solution.py
@@ -10,6 +10,7 @@
 EPS4 = 4e-06
 STEP_SIZE = 0.08
 SLOT = 32
+VMEM_LIMIT = 4 * 2**20
 
 
 def cell_terms(q, s):
@@ -195,8 +196,19 @@
     return block
 
 
-def pack_kernel(dims, q_ref, s_ref, za_ref, zb_ref, ya_ref, yb_ref, x_ref, e_ref):
-    cz, cy, cx = dims
+def pack_kernel(dims, *refs):
+    cz, cy, cx = dims
+    q_hbm, s_hbm, v_hbm, w_hbm = refs[:4]
+    q_ref, s_ref, v_ref, w_ref, za_ref, zb_ref, ya_ref, yb_ref, x_ref, e_ref = refs[4:14]
+    sems = refs[14]
+    loads = [
+        pltpu.make_async_copy(source, target, sems.at[i])
+        for i, (source, target) in enumerate(
+            ((q_hbm, q_ref), (s_hbm, s_ref), (v_hbm, v_ref), (w_hbm, w_ref))
+        )
+    ]
+    for load in loads:
+        load.start()
     half = cy // 2
     row, lane = iotas((cy, cx))
     even_z = lax.rem(lax.axis_index("gz"), 2) == 0
@@ -205,6 +217,8 @@
     top = (cz - 3) * cy
     first_a = pl.multiple_of(jnp.where(even_z, top, 0), cy)
     first_b = pl.multiple_of(jnp.where(even_z, 0, top), cy)
+    for load in loads:
+        load.wait()
     for f in range(8):
         za_ref[f] = field_of(q_ref, s_ref, 2, f, pl.ds(first_a, 3 * cy))
         zb_ref[f] = field_of(q_ref, s_ref, 2, f, pl.ds(first_b, 3 * cy))
@@ -230,21 +244,94 @@
         x_ref[f] = jnp.where(lower, blocks[f], pltpu.roll(blocks[f + 4], SLOT // 2, 1))
 
 
-def main_kernel(dims, nx, *refs):
+def stream_inner(dims, r):
+    cz, cy, cx = dims
+    for z in range(cz):
+        rows = pl.ds(z * cy, cy)
+        flux = lane_flux([field_of(r["q"], r["s"], 0, f, rows) for f in range(8)], 1)
+        for c in range(5):
+            r["out"][c, rows, :] = flux[c] - pltpu.roll(flux[c], 1, 1)
+
+
+def span(dims, r):
+    cz, cy, cx = dims
+    even_z = lax.rem(lax.axis_index("gz"), 2) == 0
+    cells = []
+    for k in range(-3, cz + 3):
+        fields = []
+        for f in range(8):
+            if k < 0:
+                rows = pl.ds((k + 3) * cy, cy)
+                v = jnp.where(even_z, r["zb"][f, rows, :], r["za"][f, rows, :])
+            elif k >= cz:
+                rows = pl.ds((k - cz) * cy, cy)
+                v = jnp.where(even_z, r["za"][f, rows, :], r["zb"][f, rows, :])
+            else:
+                v = field_of(r["q"], r["s"], 2, f, pl.ds(k * cy, cy))
+            fields.append(v)
+        cells.append(fields)
+    flux = column_fluxes(cells, 0)
+    for z in range(cz):
+        rows = pl.ds(z * cy, cy)
+        for c in range(5):
+            r["out"][c, rows, :] = flux[z + 1][c] - flux[z][c]
+
+
+def normal(dims, r):
     cz, cy, cx = dims
     half = cy // 2
-    q_ref, s_ref, v_ref, w_ref, e_ref, za_ref, zb_ref, ya_ref, yb_ref, xa_ref = refs[:10]
-    xb_ref = refs[10] if nx > 2 else xa_ref
-    state_ref, rate_ref, acc_ref = refs[-3:]
-    row, lane = iotas((cy, cx))
-    gx, gy, gz = lax.axis_index("gx"), lax.axis_index("gy"), lax.axis_index("gz")
-    even_x, even_y, even_z = lax.rem(gx, 2) == 0, lax.rem(gy, 2) == 0, lax.rem(gz, 2) == 0
+    row, _ = iotas((cy, cx))
+    gy = lax.axis_index("gy")
+    even_y = lax.rem(gy, 2) == 0
     at_wall = gy == 0
     at_top = gy == lax.axis_size("gy") - 1
-
+    even_row = (row & 1) == 0
+    wake = jnp.broadcast_to(r["w"][...] >= 0, (cy, cx))
+    walled = jnp.logical_and(at_wall, jnp.logical_not(wake))
+    ya, yb = r["ya"], r["yb"]
+    own = [
+        [field_of(r["q"], r["s"], 1, f, pl.ds(i, cy, stride=half)) for f in range(8)]
+        for i in range(half)
+    ]
+    low_cells, high_cells = [], []
+    for i in range(3):
+        low_fields, high_fields = [], []
+        for f in range(8):
+            rows = pl.ds(i * cy, cy)
+            back = pl.ds((2 - i) * cy, cy)
+            low = jnp.where(even_y, yb[f % 4, rows, :], ya[f % 4, rows, :])
+            low = jnp.where(at_wall, yb[f % 4, back, :], low)
+            high = jnp.where(even_y, ya[f % 4, rows, :], yb[f % 4, rows, :])
+            if f < 4:
+                high = pltpu.roll(high, 1, 0)
+            else:
+                low = pltpu.roll(low, cy - 1, 0)
+            solid = own[2 - i][f]
+            solid = -solid if f in (1, 2, 3) else solid
+            low = jnp.where(walled, solid, low)
+            high = jnp.where(at_top, own[half - 1][f], high)
+            low_fields.append(jnp.where(even_row, low, pltpu.roll(own[half - 3 + i][f], 1, 0)))
+            high_fields.append(jnp.where(even_row, pltpu.roll(own[i][f], cy - 1, 0), high))
+        low_cells.append(low_fields)
+        high_cells.append(high_fields)
+    flux = column_fluxes(low_cells + own + high_cells, 2)
+    for i in range(half):
+        rows = pl.ds(i, cy, stride=half)
+        for c in range(5):
+            r["out"][c, rows, :] = r["acc"][c, rows, :] + (flux[i + 1][c] - flux[i][c])
+
+
+def stream_ends(dims, r):
+    cz, cy, cx = dims
+    _, lane = iotas((cy, cx))
+    gx = lax.axis_index("gx")
+    even_x = lax.rem(gx, 2) == 0
     t = lane & (SLOT - 1)
     take_low = jnp.logical_and(t < 3, gx > 0)
-    take_high = jnp.logical_and(jnp.logical_and(t >= 15, t < 18), gx < nx - 1)
+    inside = gx < lax.axis_size("gx") - 1
+    take_high = jnp.logical_and(jnp.logical_and(t >= 15, t < 18), inside)
+    xa_ref = r["xa"]
+    xb_ref = r.get("xb", xa_ref)
     ends = []
     for f in range(8):
         xa, xb = xa_ref[f % 4], xb_ref[f % 4]
@@ -253,76 +340,26 @@
         shift_low, shift_high = (-12, 12) if f < 4 else (-28, -4)
         low = pltpu.roll(low, shift_low % cx, 1)
         high = pltpu.roll(high, shift_high % cx, 1)
-        ends.append(jnp.where(take_low, low, jnp.where(take_high, high, e_ref[f])))
+        ends.append(jnp.where(take_low, low, jnp.where(take_high, high, r["e"][f])))
     edge = lane_flux(ends, 1)
-    edge = [v - pltpu.roll(v, 1, 1) for v in edge]
+    return [v - pltpu.roll(v, 1, 1) for v in edge]
+
+
+def finish(dims, r):
+    cz, cy, cx = dims
+    edge = stream_ends(dims, r)
+    _, lane = iotas((cy, cx))
     outer = jnp.logical_or(lane < 3, lane >= cx - 3)
+    index = jnp.where(lane < 3, lane + 3, lane - (cx - 3) + 12)
     for z in range(cz):
         rows = pl.ds(z * cy, cy)
-        flux = lane_flux([field_of(q_ref, s_ref, 0, f, rows) for f in range(8)], 1)
-        index = jnp.where(lane < 3, lane + 3, lane - (cx - 3) + 12)
-        index = jnp.where(outer, index + z * SLOT, 0)
+        scale = r["v"][rows, :] * (-1.0 / 12.0)
+        spot = jnp.where(outer, index + z * SLOT, 0)
         for c in range(5):
-            inner = flux[c] - pltpu.roll(flux[c], 1, 1)
-            outside = jnp.take_along_axis(edge[c], index, axis=1)
-            acc_ref[c, rows, :] = jnp.where(outer, outside, inner)
-
-    cells = []
-    for r in range(-3, cz + 3):
-        fields = []
-        for f in range(8):
-            if r < 0:
-                rows = pl.ds((r + 3) * cy, cy)
-                v = jnp.where(even_z, zb_ref[f, rows, :], za_ref[f, rows, :])
-            elif r >= cz:
-                rows = pl.ds((r - cz) * cy, cy)
-                v = jnp.where(even_z, za_ref[f, rows, :], zb_ref[f, rows, :])
-            else:
-                v = field_of(q_ref, s_ref, 2, f, pl.ds(r * cy, cy))
-            fields.append(v)
-        cells.append(fields)
-    flux = column_fluxes(cells, 0)
-    for z in range(cz):
-        rows = pl.ds(z * cy, cy)
-        for c in range(5):
-            acc_ref[c, rows, :] += flux[z + 1][c] - flux[z][c]
-
-    even_row = (row & 1) == 0
-    wake = jnp.broadcast_to(w_ref[...] >= 0, (cy, cx))
-    own = [
-        [field_of(q_ref, s_ref, 1, f, pl.ds(r, cy, stride=half)) for f in range(8)]
-        for r in range(half)
-    ]
-    low_cells, high_cells = [], []
-    for i in range(3):
-        low_fields, high_fields = [], []
-        for f in range(8):
-            rows = pl.ds(i * cy, cy)
-            back = pl.ds((2 - i) * cy, cy)
-            normal = jnp.where(even_y, yb_ref[f % 4, rows, :], ya_ref[f % 4, rows, :])
-            mirror = yb_ref[f % 4, back, :]
-            low = jnp.where(at_wall, mirror, normal)
-            high = jnp.where(even_y, ya_ref[f % 4, rows, :], yb_ref[f % 4, rows, :])
-            if f < 4:
-                high = pltpu.roll(high, 1, 0)
-            else:
-                low = pltpu.roll(low, cy - 1, 0)
-            solid = own[2 - i][f]
-            solid = -solid if f in (1, 2, 3) else solid
-            low = jnp.where(jnp.logical_and(at_wall, jnp.logical_not(wake)), solid, low)
-            high = jnp.where(at_top, own[half - 1][f], high)
-            low_fields.append(jnp.where(even_row, low, pltpu.roll(own[half - 3 + i][f], 1, 0)))
-            high_fields.append(jnp.where(even_row, pltpu.roll(own[i][f], cy - 1, 0), high))
-        low_cells.append(low_fields)
-        high_cells.append(high_fields)
-    flux = column_fluxes(low_cells + own + high_cells, 2)
-    for r in range(half):
-        rows = pl.ds(r, cy, stride=half)
-        scale = v_ref[rows, :] * (-1.0 / 12.0)
-        for c in range(5):
-            rate = scale * (acc_ref[c, rows, :] + (flux[r + 1][c] - flux[r][c]))
-            rate_ref[c, rows, :] = rate
-            state_ref[c, rows, :] = own[r][c] + STEP_SIZE * rate
+            ends = jnp.take_along_axis(edge[c], spot, axis=1)
+            rate = scale * (r["acc"][c, rows, :] + jnp.where(outer, ends, r["inner"][c, rows, :]))
+            r["rate"][c, rows, :] = rate
+            r["state"][c, rows, :] = r["q"][c, rows, :] + STEP_SIZE * rate
 
 
 def pairs_of(count, shift, wrap):
@@ -336,6 +373,22 @@
     return found
 
 
+def stage(body, dims, inputs, outputs, flops):
+    names = tuple(inputs) + tuple(outputs)
+
+    def kernel(*refs):
+        body(dims, dict(zip(names, refs)))
+
+    moved = 4 * sum(v.size for v in tuple(inputs.values()) + tuple(outputs.values()))
+    return pl.pallas_call(
+        kernel,
+        out_shape=tuple(outputs.values()),
+        compiler_params=pltpu.CompilerParams(vmem_limit_bytes=VMEM_LIMIT),
+        cost_estimate=pl.CostEstimate(flops=flops, bytes_accessed=moved, transcendentals=0),
+        name=body.__name__,
+    )(*inputs.values())
+
+
 def local(dims, sizes, conserved, metrics, inv_volume, wake_donor):
     cz, cy, cx = dims
     nx, ny, nz = sizes
@@ -347,9 +400,14 @@
     def shape(*d):
         return jax.ShapeDtypeStruct(d, jnp.float32)
 
-    za, zb, ya, yb, x, e = pl.pallas_call(
+    q, s, v, w, za, zb, ya, yb, x, e = pl.pallas_call(
         functools.partial(pack_kernel, dims),
+        in_specs=[pl.BlockSpec(memory_space=pltpu.HBM)] * 4,
         out_shape=(
+            shape(*q.shape),
+            shape(*s.shape),
+            shape(*v.shape),
+            jax.ShapeDtypeStruct(w.shape, w.dtype),
             shape(8, 3 * cy, cx),
             shape(8, 3 * cy, cx),
             shape(4, 3 * cy, cx),
@@ -357,8 +415,10 @@
             shape(4, cy, cx),
             shape(8, cy, cx),
         ),
+        scratch_shapes=[pltpu.SemaphoreType.DMA((4,))],
+        compiler_params=pltpu.CompilerParams(vmem_limit_bytes=VMEM_LIMIT),
         name="pack",
-    )(q, s)
+    )(*[pltpu.with_memory_space_constraint(t, pltpu.HBM) for t in (q, s, v, w)])
     second = []
     for a in range(nx):
         second.append((a * ny, (nx - 1 - a) * ny))
@@ -367,15 +427,19 @@
     zb = lax.ppermute(zb, "gz", pairs_of(nz, 1, True))
     ya = lax.ppermute(ya, "gy", pairs_of(ny, 0, False))
     yb = lax.ppermute(yb, ("gx", "gy"), second)
-    ends = [lax.ppermute(x, "gx", pairs_of(nx, 0, False))]
+    ends = {"xa": lax.ppermute(x, "gx", pairs_of(nx, 0, False))}
     if nx > 2:
-        ends.append(lax.ppermute(x, "gx", pairs_of(nx, 1, False)))
-    state, rate = pl.pallas_call(
-        functools.partial(main_kernel, dims, nx),
-        out_shape=(shape(5, cz * cy, cx), shape(5, cz * cy, cx)),
-        scratch_shapes=[pltpu.VMEM((5, cz * cy, cx), jnp.float32)],
-        name="section",
-    )(q, s, v, w, e, za, zb, ya, yb, *ends)
+        ends["xb"] = lax.ppermute(x, "gx", pairs_of(nx, 1, False))
+    total = {"out": shape(*q.shape)}
+    work = cz * cy * cx * 4000
+    (inner,) = stage(stream_inner, dims, {"q": q, "s": s}, total, work)
+    zero = {"q": q, "s": s, "za": za, "zb": zb}
+    (acc,) = stage(span, dims, zero, total, work)
+    one = {"q": q, "s": s, "w": w, "ya": ya, "yb": yb, "acc": acc}
+    (acc,) = stage(normal, dims, one, total, work)
+    two = {"q": q, "v": v, "e": e, "acc": acc, "inner": inner, **ends}
+    outs = {"state": shape(*q.shape), "rate": shape(*q.shape)}
+    state, rate = stage(finish, dims, two, outs, work)
     return state.reshape(conserved.shape), rate.reshape(conserved.shape)
 
 

time: 20.5 us -> 16 us (0.78)
  waiting for transfers between devices: 3.42 us -> 0.99 us
  Pallas kernels: 5.99 us -> 4.58 us
  local copies, waits for them, and re-layouts: 0.66 us -> 0 us
    ppermute x1, waiting for transfers between devices: 3.41 us -> 0.5 us  [local(): ends = {'xa': lax.ppermute(x, 'gx', pairs_of(nx, 0, False))}]
    pallas_call x2 -> x5, Pallas kernels: 5.99 us -> 4.58 us  [the longest x4 3.4 us: stage(): pl.pallas_call(kernel, out_shape=tuple(outputs.values()), compiler_params...]
    unnamed x10 -> x0, local copies, waits for them, and re-layouts: 0.66 us -> none
    ppermute x1, waiting for transfers between devices: 0.01 us -> 0.48 us  [local(): yb = lax.ppermute(yb, ('gx', 'gy'), second)]
  transfers between devices with their start and end apart: 5 -> 5, of which waited for: 1 -> 2; matrix products, arithmetic and copies ran while one was open for 0% -> 0% of each run, Pallas kernels for 0% -> 14%
where the time goes in v3:
time: 16 us; the launch traced here: 15.8 us
  starting transfers between devices  9.58 us (60%)
  Pallas kernels  4.58 us (29%)
  waiting for transfers between devices  0.99 us (6%)
  between operations  0.68 us (4%)
    pallas_call x4, Pallas kernels, stage(): pl.pallas_call(kernel, out_shape=tuple(outputs.values()), compiler_params...  3.4 us
    ppermute x1, starting transfers between devices, local(): yb = lax.ppermute(yb, ('gx', 'gy'), second)  3.39 us
    ppermute x1, starting transfers between devices, local(): za = lax.ppermute(za, 'gz', pairs_of(nz, 0, True))  3.12 us
    ppermute x1, starting transfers between devices, local(): zb = lax.ppermute(zb, 'gz', pairs_of(nz, 1, True))  2.47 us
    pallas_call x1, Pallas kernels, local(): pl.pallas_call(functools.partial(pack_kernel, dims), in_specs=[pl.BlockSp...  1.17 us
    ppermute x1, starting transfers between devices, local(): ends = {'xa': lax.ppermute(x, 'gx', pairs_of(nx, 0, False))}  0.6 us
    ppermute x1, waiting for transfers between devices, local(): ends = {'xa': lax.ppermute(x, 'gx', pairs_of(nx, 0, False))}  0.5 us
    ppermute x1, waiting for transfers between devices, local(): yb = lax.ppermute(yb, ('gx', 'gy'), second)  0.48 us
  transfers between devices with their start and end apart: 5, of which 2 were waited for; matrix products, arithmetic and copies ran while one was open for 0% of the time, Pallas kernels for 14%

profile of v3, /device:TPU:0, one launch (start us, length us, event | category | flops | bytes accessed | tf_op | source)
XLA Modules:
  0.0 15.8 jit_solution(6047177929188540280)
XLA Ops:
  0.6 1.2 %pack.1 = (f32[5,32,128]{2,1,0:T(8,128)S(1)}, f32[9,32,128]{2,1,0:T(8,128)S(1)}, f32[32,128]{1,0:T(8,128)S(1)}, s32[1,128]{1,0:T(1,128)S(1)}, f32[8,24,128]{2,1,...) custom-call(f32[5,32,128]{2,1,0:T(8,128)} %bitcast.7, ...), custom_call_target="tpu_custom_call" | custom-call | tf_op jit(solution)/shard_map/pack/pallas_call | solution.py:403
  1.8 3.1 %collective-permute-start.2 = (f32[8,24,128]{2,1,0:T(8,128)S(1)}, f32[8,24,128]{2,1,0:T(8,128)S(1)}, u32[]{:S(2)}, u32[]{:S(2)}) collective-permute-start(f32[8,24,128]{2,1,0:T(8,128)S(1)} %get-tuple-element.21), channel_id=1, source_target_pairs={{0,1},{1,0},{2,3},{3,2},{4,5},{5,4},{6,7},{7,6},{8,9},{9,8},{10,11... | collective-permute-start | bytes 294920 | tf_op jit(solution)/shard_map/ppermute | solution.py:426
  4.9 2.5 %collective-permute-start.3 = (f32[8,24,128]{2,1,0:T(8,128)S(1)}, f32[8,24,128]{2,1,0:T(8,128)S(1)}, u32[]{:S(2)}, u32[]{:S(2)}) collective-permute-start(f32[8,24,128]{2,1,0:T(8,128)S(1)} %get-tuple-element.22), channel_id=1, source_target_pairs={{0,3},{1,2},{2,1},{3,0},{4,7},{5,6},{6,5},{7,4},{8,11},{9,10},{10,... | collective-permute-start | bytes 294920 | tf_op jit(solution)/shard_map/ppermute | solution.py:427
  7.4 0.0 collective-permute-start
  7.4 3.4 %collective-permute-start.1 = (f32[4,24,128]{2,1,0:T(8,128)S(1)}, f32[4,24,128]{2,1,0:T(8,128)S(1)}, u32[]{:S(2)}, u32[]{:S(2)}) collective-permute-start(f32[4,24,128]{2,1,0:T(8,128)S(1)} %get-tuple-element.20), channel_id=1, source_target_pairs={{0,16},{4,8},{8,4},{16,0},{20,24},{24,20},{1,17},{5,9},{9,5},{17,1... | collective-permute-start | bytes 147464 | tf_op jit(solution)/shard_map/ppermute | solution.py:429
  10.8 0.6 %collective-permute-start.4 = (f32[4,8,128]{2,1,0:T(8,128)S(1)}, f32[4,8,128]{2,1,0:T(8,128)S(1)}, u32[]{:S(2)}, u32[]{:S(2)}) collective-permute-start(f32[4,8,128]{2,1,0:T(8,128)S(1)} %get-tuple-element.23), channel_id=1, source_target_pairs={{0,16},{16,0},{1,17},{17,1},{2,18},{18,2},{3,19},{19,3},{4,20},{20... | collective-permute-start | bytes 49160 | tf_op jit(solution)/shard_map/ppermute | solution.py:430
  11.4 0.8 %stream_inner.1.refs_4_ = f32[5,32,128]{2,1,0:T(8,128)S(1)} custom-call(f32[5,32,128]{2,1,0:T(8,128)S(1)} %get-tuple-element.14.refs_0_, f32[9,32,128]{2,1,0:T(8,128)S(1)} %get-tuple-element.17.refs_1_), custom_call_target="tpu_custom_call" | custom-call | flops 16384000 | bytes 311296 | tf_op jit(solution)/shard_map/stream_inner/pallas_call | solution.py:383
  12.2 0.0 collective-permute-done.2.refs_2_
  12.2 0.0 collective-permute-done.3.refs_3_
  12.2 0.7 %span.1.refs_5_ = f32[5,32,128]{2,1,0:T(8,128)S(1)} custom-call(f32[5,32,128]{2,1,0:T(8,128)S(1)} %get-tuple-element.14.refs_0_, f32[9,32,128]{2,1,0:T(8,128)S(1)} %get-tuple-element.17.refs_1_, f32[8,24,128]{2,1,0:T(8,128)S(1)} %collective-permute-done.2.refs_2_, f32[8,24,128]{2,1,0:T(8,128)S(1)} %collective-permute-done.3.refs_3_), custom_call_target="tpu_custom_call" | custom-call | flops 16384000 | bytes 507904 | tf_op jit(solution)/shard_map/span/pallas_call | solution.py:383
  12.9 0.0 collective-permute-done.refs_3_
  12.9 0.5 %collective-permute-done.1.refs_4_ = f32[4,24,128]{2,1,0:T(8,128)S(1)} collective-permute-done((f32[4,24,128]{2,1,0:T(8,128)S(1)}, f32[4,24,128]{2,1,0:T(8,128)S(1)}, u32[]{:S(2)}, u32[]{:S(2)}) %collective-permute-start.1) | collective-permute-done | bytes 49184 | tf_op jit(solution)/shard_map/ppermute | solution.py:429
  13.4 0.7 %normal.1.refs_3_ = f32[5,32,128]{2,1,0:T(8,128)S(1)} custom-call(f32[5,32,128]{2,1,0:T(8,128)S(1)} %get-tuple-element.14.refs_0_, f32[9,32,128]{2,1,0:T(8,128)S(1)} %get-tuple-element.17.refs_1_, s32[1,128]{1,0:T(1,128)S(1)} %get-tuple-element.18.refs_2_, f32[4,24,128]{2,1,0:T(8,128)S(1)} %collective-permute-done.refs_3_, ...), custom_call_target="tpu_custom_call" | custom-call | flops 16384000 | bytes 492032 | tf_op jit(solution)/shard_map/normal/pallas_call | solution.py:383
  14.1 0.5 %collective-permute-done.4.refs_5_ = f32[4,8,128]{2,1,0:T(8,128)S(1)} collective-permute-done((f32[4,8,128]{2,1,0:T(8,128)S(1)}, f32[4,8,128]{2,1,0:T(8,128)S(1)}, u32[]{:S(2)}, u32[]{:S(2)}) %collective-permute-start.4) | collective-permute-done | bytes 16416 | tf_op jit(solution)/shard_map/ppermute | solution.py:430
  14.6 1.2 %finish.1 = (f32[5,32,128]{2,1,0:T(8,128)}, f32[5,32,128]{2,1,0:T(8,128)}) custom-call(f32[5,32,128]{2,1,0:T(8,128)S(1)} %get-tuple-element.14.refs_0_, f32[32,128]{1,0:T(8,128)S(1)} %get-tuple-element.15.refs_1_, f32[8,8,128]{2,1,0:T(8,128)S(1)} %get-tuple-element.16.refs_2_, f32[5,32,128]{2,1,0:T(8,128)S(1)} %normal.1.refs_3_, ...), custom_call_target="tpu_custom_call" | custom-call | flops 16384000 | bytes 475136 | tf_op jit(solution)/shard_map/finish/pallas_call | solution.py:383
Async XLA Ops:
  1.8 10.4 %collective-permute-start.2 = (f32[8,24,128]{2,1,0:T(8,128)S(1)}, f32[8,24,128]{2,1,0:T(8,128)S(1)}, u32[]{:S(2)}, u32[]{:S(2)}) collective-permute-start(f32[8,24,128]{2,1,0:T(8,128)S(1)} %get-tuple-element.21), channel_id=1, source_target_pairs={{0,1},{1,0},{2,3},{3,2},{4,5},{5,4},{6,7},{7,6},{8,9},{9,8},{10,11... | collective-permute-start | bytes 294920 | tf_op jit(solution)/shard_map/ppermute | solution.py:426
  4.9 7.2 %collective-permute-start.3 = (f32[8,24,128]{2,1,0:T(8,128)S(1)}, f32[8,24,128]{2,1,0:T(8,128)S(1)}, u32[]{:S(2)}, u32[]{:S(2)}) collective-permute-start(f32[8,24,128]{2,1,0:T(8,128)S(1)} %get-tuple-element.22), channel_id=1, source_target_pairs={{0,3},{1,2},{2,1},{3,0},{4,7},{5,6},{6,5},{7,4},{8,11},{9,10},{10,... | collective-permute-start | bytes 294920 | tf_op jit(solution)/shard_map/ppermute | solution.py:427
  7.4 5.5 %collective-permute-start = (f32[4,24,128]{2,1,0:T(8,128)S(1)}, f32[4,24,128]{2,1,0:T(8,128)S(1)}, u32[]{:S(2)}, u32[]{:S(2)}) collective-permute-start(f32[4,24,128]{2,1,0:T(8,128)S(1)} %get-tuple-element.19), channel_id=1, source_target_pairs={{0,4},{4,0},{8,12},{12,8},{1,5},{5,1},{9,13},{13,9},{2,6},{6,2},{1... | collective-permute-start | bytes 147464 | tf_op jit(solution)/shard_map/ppermute | solution.py:428
  7.4 6.0 %collective-permute-start.1 = (f32[4,24,128]{2,1,0:T(8,128)S(1)}, f32[4,24,128]{2,1,0:T(8,128)S(1)}, u32[]{:S(2)}, u32[]{:S(2)}) collective-permute-start(f32[4,24,128]{2,1,0:T(8,128)S(1)} %get-tuple-element.20), channel_id=1, source_target_pairs={{0,16},{4,8},{8,4},{16,0},{20,24},{24,20},{1,17},{5,9},{9,5},{17,1... | collective-permute-start | bytes 147464 | tf_op jit(solution)/shard_map/ppermute | solution.py:429
  10.8 3.8 %collective-permute-start.4 = (f32[4,8,128]{2,1,0:T(8,128)S(1)}, f32[4,8,128]{2,1,0:T(8,128)S(1)}, u32[]{:S(2)}, u32[]{:S(2)}) collective-permute-start(f32[4,8,128]{2,1,0:T(8,128)S(1)} %get-tuple-element.23), channel_id=1, source_target_pairs={{0,16},{16,0},{1,17},{17,1},{2,18},{18,2},{3,19},{19,3},{4,20},{20... | collective-permute-start | bytes 49160 | tf_op jit(solution)/shard_map/ppermute | solution.py:430
